TPU v7x, 32 devices: a whole 2x2x4 slice. The times are simulated.
32 devices in a mesh: wide: 16 (over z, x, core), lev: 2 (over y).
Axes of the slice: x: 2, y: 2, z: 4, core: 2. Of those that a mesh axis runs over, the one named last changes fastest.
Arguments:
- member_control: float32 [16, 16, 128], P('wide'), may hold values from -6 to 6
- static_control: float32 [8, 128, 1024], P('lev', 'wide'), may hold values from -6 to 6
- perturbations: bfloat16 [16, 8, 128, 1024], P(None, 'lev', 'wide'), may hold values from -6 to 6
- innovation: float32 [8, 128, 1024], P('lev', 'wide'), may hold values from -9 to 9
- diffusivity: float32 [8, 128, 1024], P('lev', 'wide'), may hold values from 0.05 to 0.15
- rows_factor: float32 [16, 16], replicated, may hold values from -1.5 to 1.5
- column_factor: float32 [128, 128], replicated, may hold values from -0.5 to 0.5
- ocean_mask: int32 [128, 1024], P('wide'), may hold values 0 or 1
- huber_blocks: int32 [8, 16, 128], P('lev', 'wide'), may hold values 0 or 1
- fold_map: int32 [1024], replicated, may hold values from 0 to 1023, as said below
Outputs:
- increment: float32 [8, 128, 1024], P('lev', 'wide')
- member_gradient: float32 [16, 16, 128], P('wide')
- static_gradient: float32 [8, 128, 1024], P('lev', 'wide')
Inputs may be any that keep to these rules, and one draw needn't show every extreme that they name: fold_map[fold_map[j]] = j and fold_map[j] != j for every column j.
All inputs are finite; a program needn't handle non-finite values. No bound on the sum of `ocean_mask` or of `huber_blocks` on one device may be relied on, other than what follows from the above.
Results may differ from a plain program's by a relative error of at most 0.0003.
Values sent between devices are 32-bit elements; how exact they have to be, the bound alone decides.
No kernel may reach another device: no remote copies, remote signals or barrier semaphores. Data moves between devices by JAX's collectives and lax.ppermute only.
A program may use at most 64 MiB of HBM per device.

v0:
```python
import jax
import jax.numpy as jnp
from jax import lax
from jax.sharding import PartitionSpec as P

REFINE = 8
STEPS = 3


HUBER_EDGE = 1.0
VERTICAL_WEIGHT = 0.5
PRECISE = lax.Precision.HIGHEST


def with_halo(array, sides, width):
    for axis, dim in sides:
        count, length = (lax.axis_size(axis), array.shape[dim])
        up = [(i, (i + 1) % count) for i in range(count - 1)]
        down = [(j, i) for i, j in up]
        last = lax.slice_in_dim(array, length - width, length, axis=dim)
        first = lax.slice_in_dim(array, 0, width, axis=dim)
        before = lax.ppermute(last, axis, up)
        after = lax.ppermute(first, axis, down)
        array = jnp.concatenate([before, array, after], axis=dim)
    return array


def smooth_fields(values, rows_factor, column_factor):
    left_done = jnp.einsum("ij,mjk->mik", rows_factor, values, precision=PRECISE)
    return jnp.einsum("mik,kl->mil", left_done, column_factor, precision=PRECISE)


def smooth_adjoint(values, rows_factor, column_factor):
    left_done = jnp.einsum("ji,mjk->mik", rows_factor, values, precision=PRECISE)
    return jnp.einsum("mik,lk->mil", left_done, column_factor, precision=PRECISE)


def interpolate(extended, refine):
    fraction = jnp.arange(refine, dtype=jnp.float32) / refine
    below_row = extended[..., :-1, None, :]
    above_row = extended[..., 1:, None, :]
    row_terms = below_row * (1.0 - fraction)[:, None] + above_row * fraction[:, None]
    dims_of = row_terms.shape
    row_terms = row_terms.reshape(dims_of[:-3] + (dims_of[-3] * refine, dims_of[-1]))
    wrapped = jnp.roll(row_terms, -1, axis=-1)
    col_terms = row_terms[..., None] * (1.0 - fraction) + wrapped[..., None] * fraction
    return col_terms.reshape(row_terms.shape[:-1] + (row_terms.shape[-1] * refine,))


def interpolate_adjoint(fine_field, refine):
    fraction = jnp.arange(refine, dtype=jnp.float32) / refine
    dims_of = fine_field.shape
    col_terms = fine_field.reshape(dims_of[:-1] + (dims_of[-1] // refine, refine))
    coarse_cols = jnp.sum(col_terms * (1.0 - fraction), axis=-1) + jnp.roll(
        jnp.sum(col_terms * fraction, axis=-1), 1, axis=-1
    )
    row_terms = coarse_cols.reshape(
        dims_of[:-2] + (dims_of[-2] // refine, refine, dims_of[-1] // refine)
    )
    below_part = jnp.sum(row_terms * (1.0 - fraction)[:, None], axis=-2)
    above_part = jnp.sum(row_terms * fraction[:, None], axis=-2)
    zero_row = jnp.zeros_like(below_part)
    return jnp.concatenate([below_part, zero_row], axis=-2) + jnp.concatenate(
        [zero_row, above_part], axis=-2
    )


def diffuse(values, diffusivity, fold_map):
    is_last = lax.axis_index("wide") == lax.axis_size("wide") - 1
    root_kappa = jnp.sqrt(diffusivity)
    for _ in range(STEPS):
        scaled = root_kappa * values
        padded = with_halo(scaled, (("wide", 1), ("lev", 0)), 1)
        folded = jnp.take(scaled[:, -1, :], fold_map, axis=1)
        padded = padded.at[1:-1, -1, :].set(jnp.where(is_last, folded, padded[1:-1, -1, :]))
        across = (
            padded[1:-1, 2:, :]
            + padded[1:-1, :-2, :]
            + jnp.roll(scaled, 1, axis=2)
            + jnp.roll(scaled, -1, axis=2)
            - 4.0 * scaled
        )
        vertical = padded[2:, 1:-1, :] + padded[:-2, 1:-1, :] - 2.0 * scaled
        values = values + root_kappa * (across + VERTICAL_WEIGHT * vertical)
    return values


def huber_weigh(increment, innovation, ocean_cells, huber_blocks):
    misfit = increment - innovation
    expanded = jnp.repeat(jnp.repeat(huber_blocks, REFINE, axis=1), REFINE, axis=2)
    weight = jnp.where(expanded == 1, HUBER_EDGE / jnp.maximum(jnp.abs(misfit), HUBER_EDGE), 1.0)
    return ocean_cells * weight * misfit


def on_device(
    member_control,
    static_control,
    perturbations,
    innovation,
    diffusivity,
    rows_factor,
    column_factor,
    ocean_mask,
    huber_blocks,
    fold_map,
):
    members = perturbations.shape[0]
    member_scale = (members - 1) ** (-0.5)
    wide_count = lax.axis_size("wide")
    smoothed = smooth_fields(member_control, rows_factor, column_factor)
    held, coarse_rows, width = smoothed.shape
    tile_rows = coarse_rows // wide_count
    main_rows = smoothed.reshape(held, wide_count, tile_rows, width)
    next_rows = jnp.concatenate([smoothed[:, tile_rows::tile_rows, :], smoothed[:, -1:, :]], axis=1)
    windows = jnp.concatenate([main_rows, next_rows[:, :, None, :]], axis=2)
    arrived = lax.all_to_all(windows, "wide", split_axis=1, concat_axis=0, tiled=True)
    extended = arrived.reshape(members, tile_rows + 1, width)
    fine_field = interpolate(extended, REFINE)
    ensemble = jnp.sum(fine_field[:, None] * perturbations, axis=0)
    ocean_cells = ocean_mask.astype(jnp.float32)
    increment = ocean_cells * (
        member_scale * ensemble + diffuse(static_control, diffusivity, fold_map)
    )
    weighted = huber_weigh(increment, innovation, ocean_cells, huber_blocks)
    static_gradient = static_control + diffuse(weighted, diffusivity, fold_map)
    fine_terms = jnp.sum(perturbations * weighted[None], axis=1) * member_scale
    level_part = interpolate_adjoint(fine_terms, REFINE)
    ext_grad = lax.psum(level_part, "lev")
    windows = lax.all_to_all(ext_grad[:, None], "wide", split_axis=0, concat_axis=1, tiled=True)
    main_rows = windows[:, :, :tile_rows, :]
    next_rows = windows[:, :, tile_rows, :]
    main_rows = main_rows.at[:, 1:, 0, :].add(next_rows[:, :-1, :])
    main_rows = main_rows.at[:, -1, tile_rows - 1, :].add(next_rows[:, -1, :])
    smooth_grad = main_rows.reshape(held, coarse_rows, width)
    member_gradient = member_control + smooth_adjoint(smooth_grad, rows_factor, column_factor)
    return (increment, member_gradient, static_gradient)


def solution(mesh):
    return jax.shard_map(
        on_device,
        mesh=mesh,
        in_specs=(
            P("wide", None, None),
            P("lev", "wide", None),
            P(None, "lev", "wide", None),
            P("lev", "wide", None),
            P("lev", "wide", None),
            P(),
            P(),
            P("wide", None),
            P("lev", "wide", None),
            P(),
        ),
        out_specs=(P("lev", "wide", None), P("wide", None, None), P("lev", "wide", None)),
        check_vma=False,
    )
```

profile of v0, /device:TPU:0, one launch (start us, length us, event | category | flops | bytes accessed | tf_op | source)
XLA Modules:
  0.0 148.4 jit_solution(14129248455665932806)
XLA Ops:
  0.6 1.0 sqrt.4
  1.6 1.1 copy_multiply_fusion.3
  2.7 1.3 collective-permute-start.1
  4.0 3.0 %collective-permute-start = (f32[4,1,1024]{2,0,1:T(4,128)S(1)}, f32[4,1,1024]{2,0,1:T(4,128)S(1)}, u32[]{:S(2)}, u32[]{:S(2)}) collective-permute-start(f32[4,1,1024]{2,0,1:T(4,128)S(1)} %get-tuple-element.178), channel_id=1, source_target_pairs={{0,2},{2,4},{4,6},{6,8},{8,10},{10,12},{12,14},{14,16},{16,18},{18... | collective-permute-start | bytes 49160 | tf_op jit(solution)/shard_map/ppermute | solution.py:22
  7.0 0.8 convolution_bitcast_fusion.2
  8.7 8.0 %all-to-all-start = ((f32[1,16,2,128]{3,2,0,1:T(2,128)}), f32[1,16,2,128]{3,2,0,1:T(2,128)S(1)}, u32[]{:S(2)}, u32[]{:S(2)}) async-start(f32[1,16,2,128]{3,2,0,1:T(2,128)} %copy.546), calls=%async_computation | async-start | bytes 32768 | tf_op jit(solution)/shard_map/all_to_all | solution.py:116
  19.2 2.8 %gather_fusion = f32[1024,4]{1,0:T(8,128)S(1)} fusion(f32[4,1024]{0,1:T(8,128)S(1)} %copy.555, s32[1024]{0:T(1024)S(1)} %fusion.62), kind=kCustom, calls=%fused_computation.clone | custom fusion | bytes 36864 | tf_op jit(solution)/shard_map/jit(_take)/gather | solution.py:74
  23.6 3.4 %collective-permute-start.2 = (f32[1,10,1024]{2,0,1:T(1,128)S(1)}, f32[1,10,1024]{2,0,1:T(1,128)S(1)}, u32[]{:S(2)}, u32[]{:S(2)}) collective-permute-start(f32[1,10,1024]{2,0,1:T(1,128)S(1)} %get-tuple-element.135), channel_id=1, source_target_pairs={{0,1},{2,3},{4,5},{6,7},{8,9},{10,11},{12,13},{14,15},{16,17},{18,... | collective-permute-start | bytes 122888 | tf_op jit(solution)/shard_map/ppermute | solution.py:22
  27.1 1.3 collective-permute-start.3
  29.4 2.4 %fusion.2 = f32[16,8,1024]{0,2,1:T(8,128)} fusion(f32[1024]{0:T(1024)S(1)} %mul.286, f32[16,8,128]{0,2,1:T(8,128)S(1)} %copy.551, f32[1024]{0:T(1024)S(1)} %mul.280, f32[16,8,128]{0,2,1:T(8,128)S(1)} %multiply_add_fusion), kind=kLoop, calls=%fused_computation.11 | loop fusion | flops 393216 | bytes 663552 | tf_op jit(solution)/shard_map/add | solution.py:46
  31.9 2.9 %copy.552 = f32[16,8,1024]{2,1,0:T(8,128)S(1)} copy(f32[16,8,1024]{0,2,1:T(8,128)} %fusion.2) | data formatting | bytes 1048576 | tf_op jit(solution)/shard_map/add | solution.py:46
  35.9 1.3 collective-permute-start.5
  37.2 3.0 %collective-permute-start.4 = (f32[4,1,1024]{2,0,1:T(4,128)S(1)}, f32[4,1,1024]{2,0,1:T(4,128)S(1)}, u32[]{:S(2)}, u32[]{:S(2)}) collective-permute-start(f32[4,1,1024]{2,0,1:T(4,128)S(1)} %get-tuple-element.171), channel_id=1, source_target_pairs={{0,2},{2,4},{4,6},{6,8},{8,10},{10,12},{12,14},{14,16},{16,18},{18... | collective-permute-start | bytes 49160 | tf_op jit(solution)/shard_map/ppermute | solution.py:22
  40.5 2.8 %gather_fusion.1 = f32[1024,4]{1,0:T(8,128)S(1)} fusion(f32[4,1024]{0,1:T(8,128)S(1)} %copy.563, s32[1024]{0:T(1024)S(1)} %fusion.62), kind=kCustom, calls=%fused_computation.1.clone | custom fusion | bytes 36864 | tf_op jit(solution)/shard_map/jit(_take)/gather | solution.py:74
  43.6 4.5 %collective-permute-start.6 = (f32[1,10,1024]{2,0,1:T(1,128)S(1)}, f32[1,10,1024]{2,0,1:T(1,128)S(1)}, u32[]{:S(2)}, u32[]{:S(2)}) collective-permute-start(f32[1,10,1024]{2,0,1:T(1,128)S(1)} %get-tuple-element.133), channel_id=1, source_target_pairs={{0,1},{2,3},{4,5},{6,7},{8,9},{10,11},{12,13},{14,15},{16,17},{18,... | collective-permute-start | bytes 122888 | tf_op jit(solution)/shard_map/ppermute | solution.py:22
  48.2 1.3 collective-permute-start.7
  49.8 4.4 %collective-permute-done.7 = f32[1,10,1024]{2,0,1:T(1,128)S(1)} collective-permute-done((f32[1,10,1024]{2,0,1:T(1,128)S(1)}, f32[1,10,1024]{2,0,1:T(1,128)S(1)}, u32[]{:S(2)}, u32[]{:S(2)}) %collective-permute-start.7) | collective-permute-done | bytes 40992 | tf_op jit(solution)/shard_map/ppermute | solution.py:23
  55.0 1.3 collective-permute-start.9
  56.3 3.0 %collective-permute-start.8 = (f32[4,1,1024]{2,0,1:T(4,128)S(1)}, f32[4,1,1024]{2,0,1:T(4,128)S(1)}, u32[]{:S(2)}, u32[]{:S(2)}) collective-permute-start(f32[4,1,1024]{2,0,1:T(4,128)S(1)} %get-tuple-element.164), channel_id=1, source_target_pairs={{0,2},{2,4},{4,6},{6,8},{8,10},{10,12},{12,14},{14,16},{16,18},{18... | collective-permute-start | bytes 49160 | tf_op jit(solution)/shard_map/ppermute | solution.py:22
  59.6 2.8 %gather_fusion.2 = f32[1024,4]{1,0:T(8,128)S(1)} fusion(f32[4,1024]{0,1:T(8,128)S(1)} %copy.570, s32[1024]{0:T(1024)S(1)} %fusion.62), kind=kCustom, calls=%fused_computation.2.clone | custom fusion | bytes 36864 | tf_op jit(solution)/shard_map/jit(_take)/gather | solution.py:74
  62.7 1.5 collective-permute-start.10
  64.2 1.3 collective-permute-start.11
  65.8 4.3 %collective-permute-done.11 = f32[1,10,1024]{2,0,1:T(1,128)S(1)} collective-permute-done((f32[1,10,1024]{2,0,1:T(1,128)S(1)}, f32[1,10,1024]{2,0,1:T(1,128)S(1)}, u32[]{:S(2)}, u32[]{:S(2)}) %collective-permute-start.11) | collective-permute-done | bytes 40992 | tf_op jit(solution)/shard_map/ppermute | solution.py:23
  72.3 2.8 %gather_fusion.3 = f32[1024,4]{1,0:T(8,128)S(1)} fusion(f32[4,1024]{0,1:T(8,128)S(1)} %copy.583, s32[1024]{0:T(1024)S(1)} %fusion.62), kind=kCustom, calls=%fused_computation.3.clone | custom fusion | bytes 36864 | tf_op jit(solution)/shard_map/jit(_take)/gather | solution.py:74
  75.3 1.3 collective-permute-start.13
  76.6 3.0 %collective-permute-start.12 = (f32[4,1,1024]{2,0,1:T(4,128)S(1)}, f32[4,1,1024]{2,0,1:T(4,128)S(1)}, u32[]{:S(2)}, u32[]{:S(2)}) collective-permute-start(f32[4,1,1024]{2,0,1:T(4,128)S(1)} %get-tuple-element.157), channel_id=1, source_target_pairs={{0,2},{2,4},{4,6},{6,8},{8,10},{10,12},{12,14},{14,16},{16,18},{18... | collective-permute-start | bytes 49160 | tf_op jit(solution)/shard_map/ppermute | solution.py:22
  79.7 2.7 %copy.577 = f32[16,8,1024]{0,2,1:T(8,128)} copy(f32[16,8,1024]{2,1,0:T(8,128)S(1)} %fusion.4) | data formatting | bytes 1048576 | tf_op jit(solution)/shard_map/reduce_sum | solution.py:126
  82.3 5.0 %fusion.1 = (f32[16,8,128]{0,2,1:T(8,128)S(1)}, f32[16,8,128]{0,2,1:T(8,128)S(1)}) fusion(f32[16,8,1024]{0,2,1:T(8,128)} %copy.577, f32[8]{0:T(128)S(1)} %get-tuple-element.185, f32[8]{0:T(128)S(1)} %get-tuple-element.186), kind=kLoop, calls=%fused_computation.9 | loop fusion | flops 491520 | bytes 655424 | tf_op jit(solution)/shard_map/reduce_sum | solution.py:55
  87.6 8.9 %psum.7 = f32[16,1,2,128]{0,3,2,1:T(8,128)S(1)} all-reduce(f32[16,1,2,128]{0,3,2,1:T(8,128)S(1)} %add_bitcast_fusion), channel_id=1, replica_groups=mesh['wide'=16,'lev'=2] {'lev'}, use_global_device_ids=true, to_apply=%region_6.8 | all-reduce | flops 4096 | bytes 32768 | tf_op jit(solution)/shard_map/psum | solution.py:128
  97.2 6.2 %all-to-all-start.1 = ((f32[16,1,2,128]{3,2,1,0:T(2,128)}), f32[16,1,2,128]{3,2,1,0:T(2,128)S(1)}, u32[]{:S(2)}, u32[]{:S(2)}) async-start(f32[16,1,2,128]{3,2,1,0:T(2,128)} %copy.578), calls=%async_computation.1 | async-start | bytes 32768 | tf_op jit(solution)/shard_map/all_to_all | solution.py:129
  103.6 3.9 %collective-permute-start.14 = (f32[1,10,1024]{2,0,1:T(1,128)S(1)}, f32[1,10,1024]{2,0,1:T(1,128)S(1)}, u32[]{:S(2)}, u32[]{:S(2)}) collective-permute-start(f32[1,10,1024]{2,0,1:T(1,128)S(1)} %get-tuple-element.129), channel_id=1, source_target_pairs={{0,1},{2,3},{4,5},{6,7},{8,9},{10,11},{12,13},{14,15},{16,17},{18,... | collective-permute-start | bytes 122888 | tf_op jit(solution)/shard_map/ppermute | solution.py:22
  107.5 1.3 collective-permute-start.15
  108.8 1.2 all-to-all-done.1
  110.6 0.8 fusion.5
  111.4 1.9 %collective-permute-done.15 = f32[1,10,1024]{2,0,1:T(1,128)S(1)} collective-permute-done((f32[1,10,1024]{2,0,1:T(1,128)S(1)}, f32[1,10,1024]{2,0,1:T(1,128)S(1)}, u32[]{:S(2)}, u32[]{:S(2)}) %collective-permute-start.15) | collective-permute-done | bytes 40992 | tf_op jit(solution)/shard_map/ppermute | solution.py:23
  114.4 1.3 collective-permute-start.17
  115.7 3.0 %collective-permute-start.16 = (f32[4,1,1024]{2,0,1:T(4,128)S(1)}, f32[4,1,1024]{2,0,1:T(4,128)S(1)}, u32[]{:S(2)}, u32[]{:S(2)}) collective-permute-start(f32[4,1,1024]{2,0,1:T(4,128)S(1)} %get-tuple-element.150), channel_id=1, source_target_pairs={{0,2},{2,4},{4,6},{6,8},{8,10},{10,12},{12,14},{14,16},{16,18},{18... | collective-permute-start | bytes 49160 | tf_op jit(solution)/shard_map/ppermute | solution.py:22
  119.1 2.8 %gather_fusion.4 = f32[1024,4]{1,0:T(8,128)S(1)} fusion(f32[4,1024]{0,1:T(8,128)S(1)} %copy.592, s32[1024]{0:T(1024)S(1)} %fusion.62), kind=kCustom, calls=%fused_computation.4.clone | custom fusion | bytes 36864 | tf_op jit(solution)/shard_map/jit(_take)/gather | solution.py:74
  122.4 2.0 %collective-permute-start.18 = (f32[1,10,1024]{2,0,1:T(1,128)S(1)}, f32[1,10,1024]{2,0,1:T(1,128)S(1)}, u32[]{:S(2)}, u32[]{:S(2)}) collective-permute-start(f32[1,10,1024]{2,0,1:T(1,128)S(1)} %get-tuple-element.127), channel_id=1, source_target_pairs={{0,1},{2,3},{4,5},{6,7},{8,9},{10,11},{12,13},{14,15},{16,17},{18,... | collective-permute-start | bytes 122888 | tf_op jit(solution)/shard_map/ppermute | solution.py:22
  124.4 1.3 collective-permute-start.19
  126.1 4.5 %collective-permute-done.19 = f32[1,10,1024]{2,0,1:T(1,128)S(1)} collective-permute-done((f32[1,10,1024]{2,0,1:T(1,128)S(1)}, f32[1,10,1024]{2,0,1:T(1,128)S(1)}, u32[]{:S(2)}, u32[]{:S(2)}) %collective-permute-start.19) | collective-permute-done | bytes 40992 | tf_op jit(solution)/shard_map/ppermute | solution.py:23
  131.5 1.3 collective-permute-start.21
  132.8 3.0 %collective-permute-start.20 = (f32[4,1,1024]{2,0,1:T(4,128)S(1)}, f32[4,1,1024]{2,0,1:T(4,128)S(1)}, u32[]{:S(2)}, u32[]{:S(2)}) collective-permute-start(f32[4,1,1024]{2,0,1:T(4,128)S(1)} %get-tuple-element.143), channel_id=1, source_target_pairs={{0,2},{2,4},{4,6},{6,8},{8,10},{10,12},{12,14},{14,16},{16,18},{18... | collective-permute-start | bytes 49160 | tf_op jit(solution)/shard_map/ppermute | solution.py:22
  136.2 2.8 %gather_fusion.5 = f32[1024,4]{1,0:T(8,128)S(1)} fusion(f32[4,1024]{0,1:T(8,128)S(1)} %copy.603, s32[1024]{0:T(1024)S(1)} %fusion.62), kind=kCustom, calls=%fused_computation.5.clone | custom fusion | bytes 36864 | tf_op jit(solution)/shard_map/jit(_take)/gather | solution.py:74
  139.5 1.5 collective-permute-start.22
  140.9 1.3 collective-permute-start.23
  142.6 4.5 %collective-permute-done.23 = f32[1,10,1024]{2,0,1:T(1,128)S(1)} collective-permute-done((f32[1,10,1024]{2,0,1:T(1,128)S(1)}, f32[1,10,1024]{2,0,1:T(1,128)S(1)}, u32[]{:S(2)}, u32[]{:S(2)}) %collective-permute-start.23) | collective-permute-done | bytes 40992 | tf_op jit(solution)/shard_map/ppermute | solution.py:23
  147.6 0.8 fusion.11
  (154 shorter events, 17.8 us)
Async XLA Ops:
  0.6 7.3 %copy-start = (f32[128,128]{1,0:T(8,128)S(1)}, f32[128,128]{1,0:T(8,128)}, u32[]{:S(2)}) copy-start(f32[128,128]{1,0:T(8,128)} %param.34) | copy-start | bytes 196612
  2.7 20.8 %collective-permute-start.1 = (f32[4,1,1024]{2,0,1:T(4,128)S(1)}, f32[4,1,1024]{2,0,1:T(4,128)S(1)}, u32[]{:S(2)}, u32[]{:S(2)}) collective-permute-start(f32[4,1,1024]{2,0,1:T(4,128)S(1)} %get-tuple-element.177), channel_id=1, source_target_pairs={{2,0},{4,2},{6,4},{8,6},{10,8},{12,10},{14,12},{16,14},{18,16},{20... | collective-permute-start | bytes 49160 | tf_op jit(solution)/shard_map/ppermute | solution.py:23
  4.0 19.5 %collective-permute-start = (f32[4,1,1024]{2,0,1:T(4,128)S(1)}, f32[4,1,1024]{2,0,1:T(4,128)S(1)}, u32[]{:S(2)}, u32[]{:S(2)}) collective-permute-start(f32[4,1,1024]{2,0,1:T(4,128)S(1)} %get-tuple-element.178), channel_id=1, source_target_pairs={{0,2},{2,4},{4,6},{6,8},{8,10},{10,12},{12,14},{14,16},{16,18},{18... | collective-permute-start | bytes 49160 | tf_op jit(solution)/shard_map/ppermute | solution.py:22
  8.7 19.7 %all-to-all-start = ((f32[1,16,2,128]{3,2,0,1:T(2,128)}), f32[1,16,2,128]{3,2,0,1:T(2,128)S(1)}, u32[]{:S(2)}, u32[]{:S(2)}) async-start(f32[1,16,2,128]{3,2,0,1:T(2,128)} %copy.546), calls=%async_computation | async-start | bytes 32768 | tf_op jit(solution)/shard_map/all_to_all | solution.py:116
  23.6 11.4 %collective-permute-start.2 = (f32[1,10,1024]{2,0,1:T(1,128)S(1)}, f32[1,10,1024]{2,0,1:T(1,128)S(1)}, u32[]{:S(2)}, u32[]{:S(2)}) collective-permute-start(f32[1,10,1024]{2,0,1:T(1,128)S(1)} %get-tuple-element.135), channel_id=1, source_target_pairs={{0,1},{2,3},{4,5},{6,7},{8,9},{10,11},{12,13},{14,15},{16,17},{18,... | collective-permute-start | bytes 122888 | tf_op jit(solution)/shard_map/ppermute | solution.py:22
  27.1 8.0 %collective-permute-start.3 = (f32[1,10,1024]{2,0,1:T(1,128)S(1)}, f32[1,10,1024]{2,0,1:T(1,128)S(1)}, u32[]{:S(2)}, u32[]{:S(2)}) collective-permute-start(f32[1,10,1024]{2,0,1:T(1,128)S(1)} %get-tuple-element.136), channel_id=1, source_target_pairs={{1,0},{3,2},{5,4},{7,6},{9,8},{11,10},{13,12},{15,14},{17,16},{19,... | collective-permute-start | bytes 122888 | tf_op jit(solution)/shard_map/ppermute | solution.py:23
  29.4 5.4 %copy-start.1 = (bf16[16,4,8,1024]{3,2,1,0:T(8,128)(2,1)S(1)}, bf16[16,4,8,1024]{3,2,1,0:T(8,128)(2,1)}, u32[]{:S(2)}) copy-start(bf16[16,4,8,1024]{3,2,1,0:T(8,128)(2,1)} %param.30) | copy-start | bytes 3145732
  31.9 3.5 %copy-start.2 = (f32[4,8,1024]{2,1,0:T(8,128)S(1)}, f32[4,8,1024]{2,1,0:T(8,128)}, u32[]{:S(2)}) copy-start(f32[4,8,1024]{2,1,0:T(8,128)} %param.29) | copy-start | bytes 393220
  35.7 35.0 %copy-start.4 = (f32[4,8,1024]{2,1,0:T(8,128)S(1)}, f32[4,8,1024]{2,1,0:T(8,128)}, u32[]{:S(2)}) copy-start(f32[4,8,1024]{2,1,0:T(8,128)} %param.31) | copy-start | bytes 393220
  35.9 7.7 %collective-permute-start.5 = (f32[4,1,1024]{2,0,1:T(4,128)S(1)}, f32[4,1,1024]{2,0,1:T(4,128)S(1)}, u32[]{:S(2)}, u32[]{:S(2)}) collective-permute-start(f32[4,1,1024]{2,0,1:T(4,128)S(1)} %get-tuple-element.170), channel_id=1, source_target_pairs={{2,0},{4,2},{6,4},{8,6},{10,8},{12,10},{14,12},{16,14},{18,16},{20... | collective-permute-start | bytes 49160 | tf_op jit(solution)/shard_map/ppermute | solution.py:23
  37.2 6.4 %collective-permute-start.4 = (f32[4,1,1024]{2,0,1:T(4,128)S(1)}, f32[4,1,1024]{2,0,1:T(4,128)S(1)}, u32[]{:S(2)}, u32[]{:S(2)}) collective-permute-start(f32[4,1,1024]{2,0,1:T(4,128)S(1)} %get-tuple-element.171), channel_id=1, source_target_pairs={{0,2},{2,4},{4,6},{6,8},{8,10},{10,12},{12,14},{14,16},{16,18},{18... | collective-permute-start | bytes 49160 | tf_op jit(solution)/shard_map/ppermute | solution.py:22
  43.6 6.2 %collective-permute-start.6 = (f32[1,10,1024]{2,0,1:T(1,128)S(1)}, f32[1,10,1024]{2,0,1:T(1,128)S(1)}, u32[]{:S(2)}, u32[]{:S(2)}) collective-permute-start(f32[1,10,1024]{2,0,1:T(1,128)S(1)} %get-tuple-element.133), channel_id=1, source_target_pairs={{0,1},{2,3},{4,5},{6,7},{8,9},{10,11},{12,13},{14,15},{16,17},{18,... | collective-permute-start | bytes 122888 | tf_op jit(solution)/shard_map/ppermute | solution.py:22
  48.2 6.0 %collective-permute-start.7 = (f32[1,10,1024]{2,0,1:T(1,128)S(1)}, f32[1,10,1024]{2,0,1:T(1,128)S(1)}, u32[]{:S(2)}, u32[]{:S(2)}) collective-permute-start(f32[1,10,1024]{2,0,1:T(1,128)S(1)} %get-tuple-element.134), channel_id=1, source_target_pairs={{1,0},{3,2},{5,4},{7,6},{9,8},{11,10},{13,12},{15,14},{17,16},{19,... | collective-permute-start | bytes 122888 | tf_op jit(solution)/shard_map/ppermute | solution.py:23
  55.0 7.7 %collective-permute-start.9 = (f32[4,1,1024]{2,0,1:T(4,128)S(1)}, f32[4,1,1024]{2,0,1:T(4,128)S(1)}, u32[]{:S(2)}, u32[]{:S(2)}) collective-permute-start(f32[4,1,1024]{2,0,1:T(4,128)S(1)} %get-tuple-element.163), channel_id=1, source_target_pairs={{2,0},{4,2},{6,4},{8,6},{10,8},{12,10},{14,12},{16,14},{18,16},{20... | collective-permute-start | bytes 49160 | tf_op jit(solution)/shard_map/ppermute | solution.py:23
  56.3 6.4 %collective-permute-start.8 = (f32[4,1,1024]{2,0,1:T(4,128)S(1)}, f32[4,1,1024]{2,0,1:T(4,128)S(1)}, u32[]{:S(2)}, u32[]{:S(2)}) collective-permute-start(f32[4,1,1024]{2,0,1:T(4,128)S(1)} %get-tuple-element.164), channel_id=1, source_target_pairs={{0,2},{2,4},{4,6},{6,8},{8,10},{10,12},{12,14},{14,16},{16,18},{18... | collective-permute-start | bytes 49160 | tf_op jit(solution)/shard_map/ppermute | solution.py:22
  62.7 3.1 %collective-permute-start.10 = (f32[1,10,1024]{2,0,1:T(1,128)S(1)}, f32[1,10,1024]{2,0,1:T(1,128)S(1)}, u32[]{:S(2)}, u32[]{:S(2)}) collective-permute-start(f32[1,10,1024]{2,0,1:T(1,128)S(1)} %get-tuple-element.131), channel_id=1, source_target_pairs={{0,1},{2,3},{4,5},{6,7},{8,9},{10,11},{12,13},{14,15},{16,17},{18,... | collective-permute-start | bytes 122888 | tf_op jit(solution)/shard_map/ppermute | solution.py:22
  64.2 5.9 %collective-permute-start.11 = (f32[1,10,1024]{2,0,1:T(1,128)S(1)}, f32[1,10,1024]{2,0,1:T(1,128)S(1)}, u32[]{:S(2)}, u32[]{:S(2)}) collective-permute-start(f32[1,10,1024]{2,0,1:T(1,128)S(1)} %get-tuple-element.132), channel_id=1, source_target_pairs={{1,0},{3,2},{5,4},{7,6},{9,8},{11,10},{13,12},{15,14},{17,16},{19,... | collective-permute-start | bytes 122888 | tf_op jit(solution)/shard_map/ppermute | solution.py:23
  75.3 28.1 %collective-permute-start.13 = (f32[4,1,1024]{2,0,1:T(4,128)S(1)}, f32[4,1,1024]{2,0,1:T(4,128)S(1)}, u32[]{:S(2)}, u32[]{:S(2)}) collective-permute-start(f32[4,1,1024]{2,0,1:T(4,128)S(1)} %get-tuple-element.156), channel_id=1, source_target_pairs={{2,0},{4,2},{6,4},{8,6},{10,8},{12,10},{14,12},{16,14},{18,16},{20... | collective-permute-start | bytes 49160 | tf_op jit(solution)/shard_map/ppermute | solution.py:23
  76.6 26.8 %collective-permute-start.12 = (f32[4,1,1024]{2,0,1:T(4,128)S(1)}, f32[4,1,1024]{2,0,1:T(4,128)S(1)}, u32[]{:S(2)}, u32[]{:S(2)}) collective-permute-start(f32[4,1,1024]{2,0,1:T(4,128)S(1)} %get-tuple-element.157), channel_id=1, source_target_pairs={{0,2},{2,4},{4,6},{6,8},{8,10},{10,12},{12,14},{14,16},{16,18},{18... | collective-permute-start | bytes 49160 | tf_op jit(solution)/shard_map/ppermute | solution.py:22
  82.3 28.1 %copy-start.6 = (f32[16,16]{1,0:T(8,128)S(1)}, f32[16,16]{1,0:T(8,128)}, u32[]{:S(2)}) copy-start(f32[16,16]{1,0:T(8,128)} %param.33) | copy-start | bytes 3076
  82.3 28.3 %copy-start.5 = (f32[1,16,128]{2,1,0:T(8,128)S(1)}, f32[1,16,128]{2,1,0:T(8,128)}, u32[]{:S(2)}) copy-start(f32[1,16,128]{2,1,0:T(8,128)} %param.28) | copy-start | bytes 24580
  87.6 43.5 %copy-start.3 = (f32[4,8,1024]{2,1,0:T(8,128)S(1)}, f32[4,8,1024]{2,1,0:T(8,128)}, u32[]{:S(2)}) copy-start(f32[4,8,1024]{2,1,0:T(8,128)} %param.32) | copy-start | bytes 393220
  97.2 12.7 %all-to-all-start.1 = ((f32[16,1,2,128]{3,2,1,0:T(2,128)}), f32[16,1,2,128]{3,2,1,0:T(2,128)S(1)}, u32[]{:S(2)}, u32[]{:S(2)}) async-start(f32[16,1,2,128]{3,2,1,0:T(2,128)} %copy.578), calls=%async_computation.1 | async-start | bytes 32768 | tf_op jit(solution)/shard_map/all_to_all | solution.py:129
  103.6 7.9 %collective-permute-start.14 = (f32[1,10,1024]{2,0,1:T(1,128)S(1)}, f32[1,10,1024]{2,0,1:T(1,128)S(1)}, u32[]{:S(2)}, u32[]{:S(2)}) collective-permute-start(f32[1,10,1024]{2,0,1:T(1,128)S(1)} %get-tuple-element.129), channel_id=1, source_target_pairs={{0,1},{2,3},{4,5},{6,7},{8,9},{10,11},{12,13},{14,15},{16,17},{18,... | collective-permute-start | bytes 122888 | tf_op jit(solution)/shard_map/ppermute | solution.py:22
  107.5 5.9 %collective-permute-start.15 = (f32[1,10,1024]{2,0,1:T(1,128)S(1)}, f32[1,10,1024]{2,0,1:T(1,128)S(1)}, u32[]{:S(2)}, u32[]{:S(2)}) collective-permute-start(f32[1,10,1024]{2,0,1:T(1,128)S(1)} %get-tuple-element.130), channel_id=1, source_target_pairs={{1,0},{3,2},{5,4},{7,6},{9,8},{11,10},{13,12},{15,14},{17,16},{19,... | collective-permute-start | bytes 122888 | tf_op jit(solution)/shard_map/ppermute | solution.py:23
  114.4 7.9 %collective-permute-start.17 = (f32[4,1,1024]{2,0,1:T(4,128)S(1)}, f32[4,1,1024]{2,0,1:T(4,128)S(1)}, u32[]{:S(2)}, u32[]{:S(2)}) collective-permute-start(f32[4,1,1024]{2,0,1:T(4,128)S(1)} %get-tuple-element.149), channel_id=1, source_target_pairs={{2,0},{4,2},{6,4},{8,6},{10,8},{12,10},{14,12},{16,14},{18,16},{20... | collective-permute-start | bytes 49160 | tf_op jit(solution)/shard_map/ppermute | solution.py:23
  115.7 6.6 %collective-permute-start.16 = (f32[4,1,1024]{2,0,1:T(4,128)S(1)}, f32[4,1,1024]{2,0,1:T(4,128)S(1)}, u32[]{:S(2)}, u32[]{:S(2)}) collective-permute-start(f32[4,1,1024]{2,0,1:T(4,128)S(1)} %get-tuple-element.150), channel_id=1, source_target_pairs={{0,2},{2,4},{4,6},{6,8},{8,10},{10,12},{12,14},{14,16},{16,18},{18... | collective-permute-start | bytes 49160 | tf_op jit(solution)/shard_map/ppermute | solution.py:22
  122.4 3.7 %collective-permute-start.18 = (f32[1,10,1024]{2,0,1:T(1,128)S(1)}, f32[1,10,1024]{2,0,1:T(1,128)S(1)}, u32[]{:S(2)}, u32[]{:S(2)}) collective-permute-start(f32[1,10,1024]{2,0,1:T(1,128)S(1)} %get-tuple-element.127), channel_id=1, source_target_pairs={{0,1},{2,3},{4,5},{6,7},{8,9},{10,11},{12,13},{14,15},{16,17},{18,... | collective-permute-start | bytes 122888 | tf_op jit(solution)/shard_map/ppermute | solution.py:22
  124.4 6.3 %collective-permute-start.19 = (f32[1,10,1024]{2,0,1:T(1,128)S(1)}, f32[1,10,1024]{2,0,1:T(1,128)S(1)}, u32[]{:S(2)}, u32[]{:S(2)}) collective-permute-start(f32[1,10,1024]{2,0,1:T(1,128)S(1)} %get-tuple-element.128), channel_id=1, source_target_pairs={{1,0},{3,2},{5,4},{7,6},{9,8},{11,10},{13,12},{15,14},{17,16},{19,... | collective-permute-start | bytes 122888 | tf_op jit(solution)/shard_map/ppermute | solution.py:23
  131.5 7.9 %collective-permute-start.21 = (f32[4,1,1024]{2,0,1:T(4,128)S(1)}, f32[4,1,1024]{2,0,1:T(4,128)S(1)}, u32[]{:S(2)}, u32[]{:S(2)}) collective-permute-start(f32[4,1,1024]{2,0,1:T(4,128)S(1)} %get-tuple-element.142), channel_id=1, source_target_pairs={{2,0},{4,2},{6,4},{8,6},{10,8},{12,10},{14,12},{16,14},{18,16},{20... | collective-permute-start | bytes 49160 | tf_op jit(solution)/shard_map/ppermute | solution.py:23
  132.8 6.6 %collective-permute-start.20 = (f32[4,1,1024]{2,0,1:T(4,128)S(1)}, f32[4,1,1024]{2,0,1:T(4,128)S(1)}, u32[]{:S(2)}, u32[]{:S(2)}) collective-permute-start(f32[4,1,1024]{2,0,1:T(4,128)S(1)} %get-tuple-element.143), channel_id=1, source_target_pairs={{0,2},{2,4},{4,6},{6,8},{8,10},{10,12},{12,14},{14,16},{16,18},{18... | collective-permute-start | bytes 49160 | tf_op jit(solution)/shard_map/ppermute | solution.py:22
  139.5 3.1 %collective-permute-start.22 = (f32[1,10,1024]{2,0,1:T(1,128)S(1)}, f32[1,10,1024]{2,0,1:T(1,128)S(1)}, u32[]{:S(2)}, u32[]{:S(2)}) collective-permute-start(f32[1,10,1024]{2,0,1:T(1,128)S(1)} %get-tuple-element.125), channel_id=1, source_target_pairs={{0,1},{2,3},{4,5},{6,7},{8,9},{10,11},{12,13},{14,15},{16,17},{18,... | collective-permute-start | bytes 122888 | tf_op jit(solution)/shard_map/ppermute | solution.py:22
  140.9 6.2 %collective-permute-start.23 = (f32[1,10,1024]{2,0,1:T(1,128)S(1)}, f32[1,10,1024]{2,0,1:T(1,128)S(1)}, u32[]{:S(2)}, u32[]{:S(2)}) collective-permute-start(f32[1,10,1024]{2,0,1:T(1,128)S(1)} %get-tuple-element.126), channel_id=1, source_target_pairs={{1,0},{3,2},{5,4},{7,6},{9,8},{11,10},{13,12},{15,14},{17,16},{19,... | collective-permute-start | bytes 122888 | tf_op jit(solution)/shard_map/ppermute | solution.py:23
where the time goes:
time: 149 us; the launch traced here: 148 us
  starting transfers between devices  64.7 us (43%)
  local copies, waits for them, and re-layouts  32 us (21%)
  waiting for transfers between devices  22.2 us (15%)
  other arithmetic  16.8 us (11%)
  blocking collectives  8.93 us (6%)
  matrix products  2.02 us (1%)
  between operations  1.71 us (1%)
    ppermute x12, starting transfers between devices, with_halo(): before = lax.ppermute(last, axis, up)  35 us
    ppermute x12, waiting for transfers between devices, with_halo(): after = lax.ppermute(first, axis, down)  19.7 us
    gather x12, local copies, waits for them, and re-layouts, diffuse(): folded = jnp.take(scaled[:, -1, :], fold_map, axis=1)  18 us
    ppermute x12, starting transfers between devices, with_halo(): after = lax.ppermute(first, axis, down)  15.5 us
    psum x1, blocking collectives, on_device(): ext_grad = lax.psum(level_part, 'lev')  8.93 us
    all_to_all x1, starting transfers between devices, on_device(): lax.all_to_all(windows, 'wide', split_axis=1, concat_axis=0, tiled=True)  7.95 us
    all_to_all x1, starting transfers between devices, on_device(): lax.all_to_all(ext_grad[:, None], 'wide', split_axis=0, concat_axis=1, ti...  6.24 us
    reduce_sum x1, other arithmetic, interpolate_adjoint(): jnp.sum(col_terms * fraction, axis=-1)  5.03 us
  transfers between devices with their start and end apart: 26, of which 10 were waited for; matrix products, arithmetic and copies ran while one was open for 26% of the time, Pallas kernels for 0%

commit v1 on v0

v1 whole, which is shorter than its diff:
```python
import functools

import jax
import jax.numpy as jnp
from jax import lax
from jax.experimental import pallas as pl
from jax.experimental.pallas import tpu as pltpu
from jax.sharding import PartitionSpec as P

STEPS = 3
HUBER_EDGE = 1.0
VERTICAL_WEIGHT = 0.5
PRECISE = lax.Precision.HIGHEST
LANES = 128
GROUP = 16
F32 = jnp.float32
BF16 = jnp.bfloat16


def dot_precise(left, right, dims=((1,), (0,))):
    return lax.dot_general(left, right, (dims, ((), ())), precision=PRECISE, preferred_element_type=F32)


def dot_split(left, right, dims=((1,), (0,))):
    high = left.astype(BF16)
    rest = left - high.astype(F32)
    middle = rest.astype(BF16)
    low = (rest - middle.astype(F32)).astype(BF16)
    parts = [
        lax.dot_general(part, right, (dims, ((), ())), preferred_element_type=F32)
        for part in (low, middle, high)
    ]
    return (parts[0] + parts[1]) + parts[2]


def iota(shape, dim):
    return lax.broadcasted_iota(jnp.int32, shape, dim)


def level_at(entry, levels, lev):
    return jnp.where(lev == 0, entry, levels - 1 - entry)


def row_plan(levels, with_kappa):
    plan = [(False, d, e) for d in range(1, STEPS + 1) for e in range(levels + STEPS - d)]
    if with_kappa:
        plan += [(True, d, e) for d in range(1, STEPS) for e in range(levels + STEPS - 1 - d)]
    return plan


def padded_rows(levels, with_kappa):
    return -(-len(row_plan(levels, with_kappa)) // 8) * 8


def start_kernel(value, kappa, member, rows_f, cols_f, swap, windows):
    levels, rows, _ = value.shape
    lev = lax.axis_index("lev")
    for j in range(STEPS):
        at = level_at(levels - 1 - j, levels, lev)
        k = kappa[at]
        swap[j * rows : (j + 1) * rows, :] = jnp.sqrt(k) * value[at]
        if j < STEPS - 1:
            swap[(STEPS + j) * rows : (STEPS + j + 1) * rows, :] = k
    coarse = rows_f.shape[0]
    shape = (2 * coarse, coarse)
    pair = iota(shape, 0)
    wanted = jnp.minimum(pair // 2 + pair % 2, coarse - 1)
    pick = jnp.where(iota(shape, 1) == wanted, 1.0, 0.0).astype(F32)
    right_done = dot_precise(member[0], cols_f[...])
    windows[...] = dot_precise(dot_precise(pick, rows_f[...]), right_done)


def pack_rows(plan, row_of, up, down, rows):
    for j, (is_kappa, d, e) in enumerate(plan):
        up[j : j + 1, :] = row_of(is_kappa, e, rows - d)
        down[j : j + 1, :] = row_of(is_kappa, e, d - 1)
    for j in range(len(plan), up.shape[0]):
        up[j : j + 1, :] = jnp.zeros((1, up.shape[1]), F32)
        down[j : j + 1, :] = jnp.zeros((1, up.shape[1]), F32)


def pack_static_kernel(value, kappa, swap, blocks, up, down, interp, huber):
    levels, rows, width = value.shape
    lev = lax.axis_index("lev")

    def row_of(is_kappa, e, r):
        if e >= levels:
            start = (e - levels + (STEPS if is_kappa else 0)) * rows
            return swap[start + r : start + r + 1, :]
        at = level_at(e, levels, lev)
        k = kappa[at, r : r + 1, :]
        return k if is_kappa else jnp.sqrt(k) * value[at, r : r + 1, :]

    pack_rows(row_plan(levels, True), row_of, up, down, rows)
    coarse = interp.shape[0]
    refine = width // coarse
    shape = (coarse, width)
    column = iota(shape, 1)
    at = iota(shape, 0)
    cell = column // refine
    fraction = (column % refine).astype(F32) * (1.0 / refine)
    following = jnp.where(cell == coarse - 1, 0, cell + 1)
    below = cell == at
    interp[...] = (
        jnp.where(below, 1.0 - fraction, 0.0) + jnp.where(following == at, fraction, 0.0)
    ).astype(BF16)
    spread = jnp.where(below, 1.0, 0.0).astype(BF16)
    huber[...] = jnp.dot(blocks[...].astype(F32).astype(BF16), spread, preferred_element_type=F32)


def pack_weighted_kernel(scaled, swap, up, down):
    levels, rows, _ = scaled.shape

    def row_of(is_kappa, e, r):
        if e >= levels:
            start = (e - levels) * rows
            return swap[start + r : start + r + 1, :]
        return scaled[e, r : r + 1, :]

    pack_rows(row_plan(levels, False), row_of, up, down, rows)


def unpack_rows(plan, state, kappa_ext, low, high, rows):
    is_first = lax.axis_index("wide") == 0
    for j, (is_kappa, d, e) in enumerate(plan):
        target = kappa_ext if is_kappa else state
        before = low[j : j + 1, :]
        target[e, 2 * rows - d : 2 * rows - d + 1, :] = jnp.where(is_first, 0.0, before)
        target[e, rows + d - 1 : rows + d, :] = high[j : j + 1, :]


def diffuse_steps(state, kappa_ext, total, fold, edge, levels, rows, width, finish):
    is_last = lax.axis_index("wide") == lax.axis_size("wide") - 1
    tiles = width // LANES
    for step in range(STEPS):
        updated = levels + STEPS - 1 - step

        @pl.when(is_last)
        def _():
            for e in range(updated):
                edge[e : e + 1, :] = state[e, rows - 1 : rows, :]
            for t in range(tiles):
                index = jnp.broadcast_to(fold[:, t * LANES : (t + 1) * LANES], (8, LANES))
                lane = lax.rem(index, LANES)
                source = lax.div(index, LANES)
                found = jnp.zeros((8, LANES), F32)
                for q in range(tiles):
                    part = jnp.take_along_axis(
                        edge[:, q * LANES : (q + 1) * LANES], lane, axis=1, mode="promise_in_bounds"
                    )
                    found = jnp.where(source == q, part, found)
                for e in range(updated):
                    state[e, rows : rows + 1, t * LANES : (t + 1) * LANES] = found[e : e + 1, :]

        below = None
        for e in range(updated):
            whole = state[e]
            with_halo = step < STEPS - 1 and e < updated - 1
            kept = 2 * rows if with_halo else rows
            here = whole[:kept]
            above = state[e + 1, :kept, :]
            vertical = above if below is None else above + below[:kept]
            across = (
                pltpu.roll(whole, 2 * rows - 1, 0)[:kept]
                + pltpu.roll(whole, 1, 0)[:kept]
                + pltpu.roll(here, width - 1, 1)
                + pltpu.roll(here, 1, 1)
            )
            change = across + VERTICAL_WEIGHT * vertical - (4.0 + 2.0 * VERTICAL_WEIGHT) * here
            below = whole
            if step < STEPS - 1:
                state[e, :kept, :] = here + kappa_ext[e, :kept, :] * change
            if e < levels:
                if step == 0:
                    total[e] = change[:rows]
                elif step < STEPS - 1:
                    total[e] = total[e] + change[:rows]
                else:
                    finish(e, total[e] + change[:rows])


def static_kernel(value, kappa, swap, low, high, fold, diffused, kappa_ext, state, total, edge):
    levels, rows, width = value.shape
    lev = lax.axis_index("lev")
    zero = jnp.zeros((rows, width), F32)
    edge[...] = jnp.zeros(edge.shape, F32)
    for e in range(levels + STEPS):
        state[e, rows:, :] = zero
        if e < levels + STEPS - 1:
            kappa_ext[e, rows:, :] = zero
        if e < levels:
            at = level_at(e, levels, lev)
            k = kappa[at]
            kappa_ext[e, :rows, :] = k
            state[e, :rows, :] = jnp.sqrt(k) * value[at]
        else:
            start = (e - levels) * rows
            state[e, :rows, :] = swap[start : start + rows, :]
            if e < levels + STEPS - 1:
                start += STEPS * rows
                kappa_ext[e, :rows, :] = swap[start : start + rows, :]
    unpack_rows(row_plan(levels, True), state, kappa_ext, low, high, rows)

    def finish(e, change):
        at = level_at(e, levels, lev)
        diffused[at] = value[at] + jnp.sqrt(kappa[at]) * change

    diffuse_steps(state, kappa_ext, total, fold, edge, levels, rows, width, finish)


def weighted_kernel(
    value, weighted, kappa, kappa_ext, scaled, swap, low, high, fold, gradient, state, ring, total, edge
):
    levels, rows, width = value.shape
    lev = lax.axis_index("lev")
    zero = jnp.zeros((rows, width), F32)
    edge[...] = jnp.zeros(edge.shape, F32)
    for e in range(levels + STEPS):
        state[e, rows:, :] = zero
        if e < levels:
            state[e, :rows, :] = scaled[e]
        else:
            start = (e - levels) * rows
            state[e, :rows, :] = swap[start : start + rows, :]
    unpack_rows(row_plan(levels, False), state, ring, low, high, rows)

    def finish(e, change):
        at = level_at(e, levels, lev)
        gradient[at] = value[at] + (weighted[at] + jnp.sqrt(kappa[at]) * change)

    diffuse_steps(state, kappa_ext, total, fold, edge, levels, rows, width, finish)


def ensemble_kernel(
    windows, interp, perturbations, diffused, innovation, kappa, mask, huber, increment, weighted, scaled, swap, coarse
):
    members, levels, rows, width = perturbations.shape
    lev = lax.axis_index("lev")
    coarse[...] = dot_split(windows[...], interp[...])
    fraction = iota((rows, width), 0).astype(F32) * (1.0 / rows)

    def add_group(first, sums):
        sums = list(sums)
        for m in range(min(GROUP, members)):
            at = first + m
            fine = (1.0 - fraction) * coarse[pl.ds(2 * at, 1), :] + fraction * coarse[pl.ds(2 * at + 1, 1), :]
            for l in range(levels):
                sums[l] = sums[l] + fine * perturbations[at, l].astype(F32)
        return tuple(sums)

    sums = tuple(jnp.zeros((rows, width), F32) for _ in range(levels))
    if members <= GROUP:
        sums = add_group(0, sums)
    else:
        sums = lax.fori_loop(0, members // GROUP, lambda g, s: add_group(g * GROUP, s), sums)
    ocean = mask[...].astype(F32)
    scale = (members - 1) ** (-0.5)
    for l in range(levels):
        grown = ocean * (scale * sums[l] + diffused[l])
        increment[l] = grown
        misfit = grown - innovation[l]
        weight = jnp.where(
            huber[l : l + 1, :] > 0.5, HUBER_EDGE / jnp.maximum(jnp.abs(misfit), HUBER_EDGE), 1.0
        )
        kept = ocean * weight * misfit
        weighted[l] = kept
        rooted = jnp.sqrt(kappa[l]) * kept
        entry = level_at(l, levels, lev)
        scaled[entry] = rooted

        @pl.when(entry > 0)
        def _():
            swap[pl.ds(pl.multiple_of((levels - 1 - entry) * rows, 8), rows), :] = rooted


def terms_kernel(perturbations, weighted, interp, sent, terms):
    members, levels, rows, width = perturbations.shape
    group = min(GROUP, members)
    scale = (members - 1) ** (-0.5)
    shape = (4 * group, group * rows)
    pair = iota(shape, 0)
    column = iota(shape, 1)
    fraction = (column % rows).astype(F32) * (1.0 / rows)
    share = jnp.where(pair % 2 == 0, 1.0 - fraction, fraction)
    share = jnp.where(column // rows == pair // 4, share, 0.0)
    held = [weighted[l] for l in range(levels)]

    def one_group(first):
        for m in range(group):
            term = held[0] * perturbations[first + m, 0].astype(F32)
            for l in range(1, levels):
                term = term + held[l] * perturbations[first + m, l].astype(F32)
            terms[m * rows : (m + 1) * rows, :] = term
        narrow = dot_split(terms[...], interp[...], ((1,), (1,)))
        sent[pl.ds(pl.multiple_of(4 * first, 8), 4 * group), :] = scale * dot_precise(share, narrow)

    if members <= GROUP:
        one_group(0)
    else:
        lax.fori_loop(0, members // GROUP, lambda g, c: (one_group(g * GROUP), c)[1], 0)


def member_kernel(received, member, rows_f, cols_f, gradient):
    coarse = rows_f.shape[0]
    shape = (coarse, received.shape[0])
    source = iota(shape, 1)
    wanted = jnp.minimum(source // 4 + source % 2, coarse - 1)
    gather = jnp.where(iota(shape, 0) == wanted, 1.0, 0.0).astype(F32)
    smooth = dot_precise(gather, received[...])
    right_done = dot_precise(smooth, cols_f[...], ((1,), (1,)))
    gradient[0] = member[0] + dot_precise(rows_f[...], right_done, ((0,), (0,)))


def call(kernel, outs, scratch=(), name=None, flops=100000):
    return pl.pallas_call(
        kernel,
        out_shape=[jax.ShapeDtypeStruct(shape, dtype) for shape, dtype in outs],
        scratch_shapes=[pltpu.VMEM(shape, dtype) for shape, dtype in scratch],
        cost_estimate=pl.CostEstimate(flops=flops, transcendentals=0, bytes_accessed=0),
        name=name,
    )


def on_device(
    member_control,
    static_control,
    perturbations,
    innovation,
    diffusivity,
    rows_factor,
    column_factor,
    ocean_mask,
    huber_blocks,
    fold_map,
):
    members, levels, rows, width = perturbations.shape
    wide, lev = lax.axis_size("wide"), lax.axis_size("lev")
    coarse_rows, coarse = rows_factor.shape[0], column_factor.shape[0]
    assert lev == 2 and members == wide and coarse_rows == wide and rows == 8 and levels >= STEPS
    ring_up = [(i, (i + 1) % wide) for i in range(wide)]
    ring_down = [(j, i) for i, j in ring_up]
    partner = [(0, 1), (1, 0)]
    cell = (levels, rows, width)
    fold = fold_map.reshape(1, width)
    blocks = huber_blocks.reshape(levels, coarse)

    swap, windows = call(
        start_kernel,
        [(((2 * STEPS - 1) * rows, width), F32), ((2 * coarse_rows, coarse), F32)],
        name="start",
    )(static_control, diffusivity, member_control, rows_factor, column_factor)
    swap = lax.ppermute(swap, "lev", partner)
    windows = lax.all_to_all(windows.reshape(wide, 2, coarse), "wide", 0, 0, tiled=True)
    windows = windows.reshape(2 * members, coarse)
    count = padded_rows(levels, True)
    up, down, interp, huber = call(
        pack_static_kernel,
        [((count, width), F32), ((count, width), F32), ((coarse, width), BF16), ((levels, width), F32)],
        name="pack_static",
    )(static_control, diffusivity, swap, blocks)
    low = lax.ppermute(up, "wide", ring_up)
    high = lax.ppermute(down, "wide", ring_down)
    entries = levels + STEPS
    diffused, kappa_ext = call(
        static_kernel,
        [(cell, F32), ((entries - 1, 2 * rows, width), F32)],
        [((entries, 2 * rows, width), F32), (cell, F32), ((8, width), F32)],
        name="diffuse_static",
    )(static_control, diffusivity, swap, low, high, fold)
    increment, weighted, scaled, swap = call(
        ensemble_kernel,
        [(cell, F32), (cell, F32), (cell, F32), ((STEPS * rows, width), F32)],
        [((2 * members, width), F32)],
        name="ensemble",
    )(windows, interp, perturbations, diffused, innovation, diffusivity, ocean_mask, huber)
    swap = lax.ppermute(swap, "lev", partner)
    (sent,) = call(
        terms_kernel,
        [((4 * members, coarse), F32)],
        [((min(GROUP, members) * rows, width), F32)],
        name="terms",
    )(perturbations, weighted, interp)
    received = lax.all_to_all(
        sent.reshape(2 * members, 2, coarse), ("wide", "lev"), 0, 0, tiled=True
    ).reshape(4 * members, coarse)
    count = padded_rows(levels, False)
    up, down = call(
        pack_weighted_kernel,
        [((count, width), F32), ((count, width), F32)],
        name="pack_weighted",
    )(scaled, swap)
    low = lax.ppermute(up, "wide", ring_up)
    high = lax.ppermute(down, "wide", ring_down)
    (static_gradient,) = call(
        weighted_kernel,
        [(cell, F32)],
        [((entries, 2 * rows, width), F32), ((8, LANES), F32), (cell, F32), ((8, width), F32)],
        name="diffuse_weighted",
    )(static_control, weighted, diffusivity, kappa_ext, scaled, swap, low, high, fold)
    (member_gradient,) = call(member_kernel, [(member_control.shape, F32)], name="member")(
        received, member_control, rows_factor, column_factor
    )
    return (increment, member_gradient, static_gradient)


def solution(mesh):
    return jax.shard_map(
        on_device,
        mesh=mesh,
        in_specs=(
            P("wide", None, None),
            P("lev", "wide", None),
            P(None, "lev", "wide", None),
            P("lev", "wide", None),
            P("lev", "wide", None),
            P(),
            P(),
            P("wide", None),
            P("lev", "wide", None),
            P(),
        ),
        out_specs=(P("lev", "wide", None), P("wide", None, None), P("lev", "wide", None)),
        check_vma=False,
    )
```

time: 149 us -> 60.7 us (0.41)
  starting transfers between devices: 64.7 us -> 17.1 us
  local copies, waits for them, and re-layouts: 32 us -> 3.18 us
  Pallas kernels: 0 us -> 18.2 us
  other arithmetic: 16.8 us -> 0 us
  waiting for transfers between devices: 22.2 us -> 10.7 us
  matrix products: 2.02 us -> 0 us
    ppermute x24 -> x6, starting transfers between devices: 50.5 us -> 13.6 us  [the longest x2 8.88 us: on_device(): high = lax.ppermute(down, 'wide', ring_down)]
    pallas_call x0 -> x8, Pallas kernels: none -> 18.2 us  [the longest x1 2.85 us: on_device(): call(ensemble_kernel, [(cell, F32), (cell, F32), (cell, F32), ((STEPS * r...]
    gather x12 -> x0, local copies, waits for them, and re-layouts: 18 us -> none  [diffuse(): folded = jnp.take(scaled[:, -1, :], fold_map, axis=1)]
    ppermute x24 -> x6, waiting for transfers between devices: 21.1 us -> 7.5 us  [the longest x2 7.49 us: on_device(): swap = lax.ppermute(swap, 'lev', partner)]
    all_to_all x2 -> x1, starting transfers between devices: 14.2 us -> 3.5 us  [on_device(): lax.all_to_all(windows.reshape(wide, 2, coarse), 'wide', 0, 0, tiled=True)]
    all_to_all x0 -> x1, blocking collectives: none -> 10.4 us  [on_device(): lax.all_to_all(sent.reshape(2 * members, 2, coarse), ('wide', 'lev'), 0,...]
    psum x1 -> x0, blocking collectives: 8.93 us -> none  [on_device(): ext_grad = lax.psum(level_part, 'lev')]
    reduce_sum x4 -> x0, other arithmetic: 5.66 us -> none  [the longest x1 5.03 us: interpolate_adjoint(): jnp.sum(col_terms * fraction, axis=-1)]
  transfers between devices with their start and end apart: 26 -> 7, of which waited for: 10 -> 3; matrix products, arithmetic and copies ran while one was open for 26% -> 0% of each run, Pallas kernels for 0% -> 12%
where the time goes in v1:
time: 60.7 us; the launch traced here: 60.3 us
  Pallas kernels  18.2 us (30%)
  starting transfers between devices  17.1 us (28%)
  waiting for transfers between devices  10.7 us (18%)
  blocking collectives  10.4 us (17%)
  local copies, waits for them, and re-layouts  3.18 us (5%)
  between operations  0.7 us (1%)
    all_to_all x1, blocking collectives, on_device(): lax.all_to_all(sent.reshape(2 * members, 2, coarse), ('wide', 'lev'), 0,...  10.4 us
    ppermute x2, starting transfers between devices, on_device(): high = lax.ppermute(down, 'wide', ring_down)  8.88 us
    ppermute x2, waiting for transfers between devices, on_device(): swap = lax.ppermute(swap, 'lev', partner)  7.49 us
    ppermute x2, starting transfers between devices, on_device(): swap = lax.ppermute(swap, 'lev', partner)  4.74 us
    all_to_all x1, starting transfers between devices, on_device(): lax.all_to_all(windows.reshape(wide, 2, coarse), 'wide', 0, 0, tiled=True)  3.5 us
    all_to_all x1, waiting for transfers between devices, on_device(): lax.all_to_all(windows.reshape(wide, 2, coarse), 'wide', 0, 0, tiled=True)  3.18 us
    unnamed x14, local copies, waits for them, and re-layouts  3.18 us
    pallas_call x1, Pallas kernels, on_device(): call(ensemble_kernel, [(cell, F32), (cell, F32), (cell, F32), ((STEPS * r...  2.85 us
  transfers between devices with their start and end apart: 7, of which 3 were waited for; matrix products, arithmetic and copies ran while one was open for 0% of the time, Pallas kernels for 12%

profile of v1, /device:TPU:0, one launch (start us, length us, event | category | flops | bytes accessed | tf_op | source)
XLA Modules:
  0.0 60.3 jit_solution(896436919541652500)
XLA Ops:
  0.6 2.0 %start.1 = (f32[40,1024]{1,0:T(8,128)}, f32[32,128]{1,0:T(8,128)}) custom-call(f32[4,8,1024]{2,1,0:T(8,128)} %value.7, f32[4,8,1024]{2,1,0:T(8,128)} %kappa.9, f32[1,16,128]{2,1,0:T(8,128)} %member.5, f32[16,16]{1,0:T(8,128)} %rows_f.3, f32[128,128]{1,0:T(8,128)} %cols_f.3), custom_call_target="tpu_custom_call" | custom-call | flops 100000 | tf_op jit(solution)/shard_map/start/pallas_call | solution.py:347
  2.6 3.0 %collective-permute-start = (f32[40,1024]{1,0:T(8,128)}, f32[40,1024]{1,0:T(8,128)S(1)}, u32[]{:S(2)}, u32[]{:S(2)}) collective-permute-start(f32[40,1024]{1,0:T(8,128)} %get-tuple-element.18), channel_id=1, source_target_pairs={{0,1},{1,0},{2,3},{3,2},{4,5},{5,4},{6,7},{7,6},{8,9},{9,8},{10,11... | collective-permute-start | bytes 491528 | tf_op jit(solution)/shard_map/ppermute | solution.py:352
  5.6 4.4 %collective-permute-done.swap = f32[40,1024]{1,0:T(8,128)S(1)} collective-permute-done((f32[40,1024]{1,0:T(8,128)}, f32[40,1024]{1,0:T(8,128)S(1)}, u32[]{:S(2)}, u32[]{:S(2)}) %collective-permute-start) | collective-permute-done | bytes 163872 | tf_op jit(solution)/shard_map/ppermute | solution.py:352
  10.0 0.0 copy-start
  10.0 0.7 %copy-done = f32[40,1024]{1,0:T(8,128)} copy-done((f32[40,1024]{1,0:T(8,128)}, f32[40,1024]{1,0:T(8,128)S(1)}, u32[]{:S(2)}) %copy-start) | copy-done | bytes 163864
  10.7 1.9 %pack_static.1 = (f32[24,1024]{1,0:T(8,128)}, f32[24,1024]{1,0:T(8,128)}, bf16[128,1024]{1,0:T(8,128)(2,1)}, f32[4,1024]{1,0:T(4,128)}) custom-call(f32[4,8,1024]{2,1,0:T(8,128)} %value.7, f32[4,8,1024]{2,1,0:T(8,128)} %kappa.9, f32[40,1024]{1,0:T(8,128)} %copy-done, s32[4,128]{1,0:T(4,128)} %bitcast.11), custom_call_target="tpu_custom_call" | custom-call | flops 100000 | tf_op jit(solution)/shard_map/pack_static/pallas_call | solution.py:356
  12.6 0.0 collective-permute-start.1
  12.6 4.4 %collective-permute-start.2 = (f32[24,1024]{1,0:T(8,128)}, f32[24,1024]{1,0:T(8,128)S(1)}, u32[]{:S(2)}, u32[]{:S(2)}) collective-permute-start(f32[24,1024]{1,0:T(8,128)} %get-tuple-element.21), channel_id=1, source_target_pairs={{2,0},{4,2},{6,4},{8,6},{10,8},{12,10},{14,12},{16,14},{18,16},{20... | collective-permute-start | bytes 294920 | tf_op jit(solution)/shard_map/ppermute | solution.py:362
  17.0 3.5 %all-to-all-start = ((f32[16,2,128]{2,1,0:T(2,128)}), f32[16,2,128]{2,1,0:T(2,128)S(1)}, u32[]{:S(2)}, u32[]{:S(2)}) async-start(f32[16,2,128]{2,1,0:T(2,128)} %bitcast), calls=%async_computation | async-start | bytes 32768 | tf_op jit(solution)/shard_map/all_to_all | solution.py:353
  20.5 0.0 collective-permute-done.1.low
  20.5 0.0 copy-start.2
  20.5 0.0 collective-permute-done.2.high
  20.6 0.0 copy-start.3
  20.6 0.6 %copy-done.2 = f32[24,1024]{1,0:T(8,128)} copy-done((f32[24,1024]{1,0:T(8,128)}, f32[24,1024]{1,0:T(8,128)S(1)}, u32[]{:S(2)}) %copy-start.2) | copy-done | bytes 98328
  21.2 0.0 copy-done.3
  21.2 2.6 %diffuse_static.1 = (f32[4,8,1024]{2,1,0:T(8,128)}, f32[6,16,1024]{2,1,0:T(8,128)}) custom-call(f32[4,8,1024]{2,1,0:T(8,128)} %value.7, f32[4,8,1024]{2,1,0:T(8,128)} %kappa.9, f32[40,1024]{1,0:T(8,128)} %copy-done, f32[24,1024]{1,0:T(8,128)} %copy-done.2, f32[24,1024]{1,0:T(8,128)} %copy-done.3, s32[1,1024]{1,0:T(1,128)} %bitcast.9), custom_call_target="tpu_custom_call" | custom-call | flops 100000 | tf_op jit(solution)/shard_map/diffuse_static/pallas_call | solution.py:364
  23.8 3.2 %all-to-all-done = f32[16,2,128]{2,1,0:T(2,128)S(1)} async-done(((f32[16,2,128]{2,1,0:T(2,128)}), f32[16,2,128]{2,1,0:T(2,128)S(1)}, u32[]{:S(2)}, u32[]{:S(2)}) %all-to-all-start) | async-done | bytes 16416 | tf_op jit(solution)/shard_map/all_to_all | solution.py:353
  27.0 0.0 copy-start.4
  27.0 0.6 copy-done.4
  27.6 2.8 %ensemble.1 = (f32[4,8,1024]{2,1,0:T(8,128)}, f32[4,8,1024]{2,1,0:T(8,128)}, f32[4,8,1024]{2,1,0:T(8,128)}, f32[24,1024]{1,0:T(8,128)}) custom-call(f32[32,128]{1,0:T(8,128)} %bitcast.8, bf16[128,1024]{1,0:T(8,128)(2,1)} %get-tuple-element.19.interp, bf16[16,4,8,1024]{3,2,1,0:T(8,128)(2,1)} %perturbations.3, f32[4,8,1024]{2,1,0:T(8,128)} %get-tuple-element.22.diffused, ...), custom_call_target="tpu_custom_call" | custom-call | flops 100000 | tf_op jit(solution)/shard_map/ensemble/pallas_call | solution.py:370
  30.4 1.7 %collective-permute-start.3 = (f32[24,1024]{1,0:T(8,128)}, f32[24,1024]{1,0:T(8,128)S(1)}, u32[]{:S(2)}, u32[]{:S(2)}) collective-permute-start(f32[24,1024]{1,0:T(8,128)} %get-tuple-element.28), channel_id=1, source_target_pairs={{0,1},{1,0},{2,3},{3,2},{4,5},{5,4},{6,7},{7,6},{8,9},{9,8},{10,11... | collective-permute-start | bytes 294920 | tf_op jit(solution)/shard_map/ppermute | solution.py:376
  32.2 3.1 %collective-permute-done.3.swap = f32[24,1024]{1,0:T(8,128)S(1)} collective-permute-done((f32[24,1024]{1,0:T(8,128)}, f32[24,1024]{1,0:T(8,128)S(1)}, u32[]{:S(2)}, u32[]{:S(2)}) %collective-permute-start.3) | collective-permute-done | bytes 98336 | tf_op jit(solution)/shard_map/ppermute | solution.py:376
  35.3 0.0 copy-start.1
  35.3 0.6 %copy-done.1 = f32[24,1024]{1,0:T(8,128)} copy-done((f32[24,1024]{1,0:T(8,128)}, f32[24,1024]{1,0:T(8,128)S(1)}, u32[]{:S(2)}) %copy-start.1) | copy-done | bytes 98328
  35.9 1.6 %pack_weighted.1 = (f32[16,1024]{1,0:T(8,128)}, f32[16,1024]{1,0:T(8,128)}) custom-call(f32[4,8,1024]{2,1,0:T(8,128)} %get-tuple-element.27.scaled, f32[24,1024]{1,0:T(8,128)} %copy-done.1), custom_call_target="tpu_custom_call" | custom-call | flops 100000 | tf_op jit(solution)/shard_map/pack_weighted/pallas_call | solution.py:387
  37.5 0.0 collective-permute-start.4
  37.5 4.4 %collective-permute-start.5 = (f32[16,1024]{1,0:T(8,128)}, f32[16,1024]{1,0:T(8,128)S(1)}, u32[]{:S(2)}, u32[]{:S(2)}) collective-permute-start(f32[16,1024]{1,0:T(8,128)} %get-tuple-element.30), channel_id=1, source_target_pairs={{2,0},{4,2},{6,4},{8,6},{10,8},{12,10},{14,12},{16,14},{18,16},{20... | collective-permute-start | bytes 196616 | tf_op jit(solution)/shard_map/ppermute | solution.py:393
  42.0 2.7 %terms.1 = f32[64,128]{1,0:T(8,128)} custom-call(bf16[16,4,8,1024]{3,2,1,0:T(8,128)(2,1)} %perturbations.3, f32[4,8,1024]{2,1,0:T(8,128)} %get-tuple-element.25.weighted, bf16[128,1024]{1,0:T(8,128)(2,1)} %get-tuple-element.19.interp), custom_call_target="tpu_custom_call" | custom-call | flops 100000 | tf_op jit(solution)/shard_map/terms/pallas_call | solution.py:377
  44.6 10.4 %all_to_all.10 = f32[32,2,128]{2,1,0:T(2,128)} all-to-all(f32[32,2,128]{2,1,0:T(2,128)} %bitcast.6), channel_id=1, replica_groups=mesh['wide'=16,'lev'=2] {'wide','lev'}, dimensions={0} | all-to-all | bytes 65536 | tf_op jit(solution)/shard_map/all_to_all | solution.py:383
  55.0 2.0 %member.4 = f32[1,16,128]{2,1,0:T(8,128)} custom-call(f32[64,128]{1,0:T(8,128)} %bitcast.7, f32[1,16,128]{2,1,0:T(8,128)} %member.5, f32[16,16]{1,0:T(8,128)} %rows_f.3, f32[128,128]{1,0:T(8,128)} %cols_f.3), custom_call_target="tpu_custom_call" | custom-call | flops 100000 | tf_op jit(solution)/shard_map/member/pallas_call | solution.py:400
  57.1 0.0 collective-permute-done.4.low
  57.1 0.0 copy-start.5
  57.1 0.0 collective-permute-done.5.high
  57.1 0.0 copy-start.6
  57.1 0.6 copy-done.5
  57.7 0.0 copy-done.6
  57.7 2.6 %diffuse_weighted.1 = f32[4,8,1024]{2,1,0:T(8,128)} custom-call(f32[4,8,1024]{2,1,0:T(8,128)} %value.7, f32[4,8,1024]{2,1,0:T(8,128)} %get-tuple-element.25.weighted, f32[4,8,1024]{2,1,0:T(8,128)} %kappa.9, f32[6,16,1024]{2,1,0:T(8,128)} %get-tuple-element.26.kappa_ext, f32[4,8,1024]{2,1,0:T(8,128)} %get-tuple-element.27.scaled, f32[24,1024]{1,0:T(8,128)} %copy-done.1, ...), custom_call_target="tpu_custom_call" | custom-call | flops 100000 | tf_op jit(solution)/shard_map/diffuse_weighted/pallas_call | solution.py:394
Async XLA Ops:
  2.6 7.4 %collective-permute-start = (f32[40,1024]{1,0:T(8,128)}, f32[40,1024]{1,0:T(8,128)S(1)}, u32[]{:S(2)}, u32[]{:S(2)}) collective-permute-start(f32[40,1024]{1,0:T(8,128)} %get-tuple-element.18), channel_id=1, source_target_pairs={{0,1},{1,0},{2,3},{3,2},{4,5},{5,4},{6,7},{7,6},{8,9},{9,8},{10,11... | collective-permute-start | bytes 491528 | tf_op jit(solution)/shard_map/ppermute | solution.py:352
  10.0 0.7 %copy-start = (f32[40,1024]{1,0:T(8,128)}, f32[40,1024]{1,0:T(8,128)S(1)}, u32[]{:S(2)}) copy-start(f32[40,1024]{1,0:T(8,128)S(1)} %collective-permute-done.swap) | copy-start | bytes 491524
  12.6 8.0 %collective-permute-start.1 = (f32[24,1024]{1,0:T(8,128)}, f32[24,1024]{1,0:T(8,128)S(1)}, u32[]{:S(2)}, u32[]{:S(2)}) collective-permute-start(f32[24,1024]{1,0:T(8,128)} %get-tuple-element.20), channel_id=1, source_target_pairs={{0,2},{2,4},{4,6},{6,8},{8,10},{10,12},{12,14},{14,16},{16,18},{18... | collective-permute-start | bytes 294920 | tf_op jit(solution)/shard_map/ppermute | solution.py:361
  12.6 8.0 %collective-permute-start.2 = (f32[24,1024]{1,0:T(8,128)}, f32[24,1024]{1,0:T(8,128)S(1)}, u32[]{:S(2)}, u32[]{:S(2)}) collective-permute-start(f32[24,1024]{1,0:T(8,128)} %get-tuple-element.21), channel_id=1, source_target_pairs={{2,0},{4,2},{6,4},{8,6},{10,8},{12,10},{14,12},{16,14},{18,16},{20... | collective-permute-start | bytes 294920 | tf_op jit(solution)/shard_map/ppermute | solution.py:362
  17.0 10.0 %all-to-all-start = ((f32[16,2,128]{2,1,0:T(2,128)}), f32[16,2,128]{2,1,0:T(2,128)S(1)}, u32[]{:S(2)}, u32[]{:S(2)}) async-start(f32[16,2,128]{2,1,0:T(2,128)} %bitcast), calls=%async_computation | async-start | bytes 32768 | tf_op jit(solution)/shard_map/all_to_all | solution.py:353
  20.5 0.6 %copy-start.2 = (f32[24,1024]{1,0:T(8,128)}, f32[24,1024]{1,0:T(8,128)S(1)}, u32[]{:S(2)}) copy-start(f32[24,1024]{1,0:T(8,128)S(1)} %collective-permute-done.1.low) | copy-start | bytes 294916
  20.6 0.7 %copy-start.3 = (f32[24,1024]{1,0:T(8,128)}, f32[24,1024]{1,0:T(8,128)S(1)}, u32[]{:S(2)}) copy-start(f32[24,1024]{1,0:T(8,128)S(1)} %collective-permute-done.2.high) | copy-start | bytes 294916
  27.0 0.6 copy-start.4
  30.4 4.8 %collective-permute-start.3 = (f32[24,1024]{1,0:T(8,128)}, f32[24,1024]{1,0:T(8,128)S(1)}, u32[]{:S(2)}, u32[]{:S(2)}) collective-permute-start(f32[24,1024]{1,0:T(8,128)} %get-tuple-element.28), channel_id=1, source_target_pairs={{0,1},{1,0},{2,3},{3,2},{4,5},{5,4},{6,7},{7,6},{8,9},{9,8},{10,11... | collective-permute-start | bytes 294920 | tf_op jit(solution)/shard_map/ppermute | solution.py:376
  35.3 0.6 %copy-start.1 = (f32[24,1024]{1,0:T(8,128)}, f32[24,1024]{1,0:T(8,128)S(1)}, u32[]{:S(2)}) copy-start(f32[24,1024]{1,0:T(8,128)S(1)} %collective-permute-done.3.swap) | copy-start | bytes 294916
  37.5 19.5 %collective-permute-start.4 = (f32[16,1024]{1,0:T(8,128)}, f32[16,1024]{1,0:T(8,128)S(1)}, u32[]{:S(2)}, u32[]{:S(2)}) collective-permute-start(f32[16,1024]{1,0:T(8,128)} %get-tuple-element.29), channel_id=1, source_target_pairs={{0,2},{2,4},{4,6},{6,8},{8,10},{10,12},{12,14},{14,16},{16,18},{18... | collective-permute-start | bytes 196616 | tf_op jit(solution)/shard_map/ppermute | solution.py:392
  37.5 19.5 %collective-permute-start.5 = (f32[16,1024]{1,0:T(8,128)}, f32[16,1024]{1,0:T(8,128)S(1)}, u32[]{:S(2)}, u32[]{:S(2)}) collective-permute-start(f32[16,1024]{1,0:T(8,128)} %get-tuple-element.30), channel_id=1, source_target_pairs={{2,0},{4,2},{6,4},{8,6},{10,8},{12,10},{14,12},{16,14},{18,16},{20... | collective-permute-start | bytes 196616 | tf_op jit(solution)/shard_map/ppermute | solution.py:393
  57.1 0.6 %copy-start.5 = (f32[16,1024]{1,0:T(8,128)}, f32[16,1024]{1,0:T(8,128)S(1)}, u32[]{:S(2)}) copy-start(f32[16,1024]{1,0:T(8,128)S(1)} %collective-permute-done.4.low) | copy-start | bytes 196612
  57.1 0.6 %copy-start.6 = (f32[16,1024]{1,0:T(8,128)}, f32[16,1024]{1,0:T(8,128)S(1)}, u32[]{:S(2)}) copy-start(f32[16,1024]{1,0:T(8,128)S(1)} %collective-permute-done.5.high) | copy-start | bytes 196612

commit v2 on v1

--- a/solution.py
+++ b/solution.py
@@ -1,5 +1,3 @@
-import functools
-
 import jax
 import jax.numpy as jnp
 from jax import lax
@@ -7,12 +5,14 @@
 from jax.experimental.pallas import tpu as pltpu
 from jax.sharding import PartitionSpec as P
 
+
 STEPS = 3
 HUBER_EDGE = 1.0
 VERTICAL_WEIGHT = 0.5
 PRECISE = lax.Precision.HIGHEST
 LANES = 128
 GROUP = 16
+VMEM_BYTES = 32 * 2**20
 F32 = jnp.float32
 BF16 = jnp.bfloat16
 
@@ -21,16 +21,16 @@
     return lax.dot_general(left, right, (dims, ((), ())), precision=PRECISE, preferred_element_type=F32)
 
 
-def dot_split(left, right, dims=((1,), (0,))):
-    high = left.astype(BF16)
-    rest = left - high.astype(F32)
+def sum_parts(array, product):
+    high = array.astype(BF16)
+    rest = array - high.astype(F32)
     middle = rest.astype(BF16)
     low = (rest - middle.astype(F32)).astype(BF16)
-    parts = [
-        lax.dot_general(part, right, (dims, ((), ())), preferred_element_type=F32)
-        for part in (low, middle, high)
-    ]
-    return (parts[0] + parts[1]) + parts[2]
+    return (product(low) + product(middle)) + product(high)
+
+
+def dot_split(left, right, dims=((1,), (0,))):
+    return sum_parts(left, lambda part: lax.dot_general(part, right, (dims, ((), ())), preferred_element_type=F32))
 
 
 def iota(shape, dim):
@@ -52,22 +52,31 @@
     return -(-len(row_plan(levels, with_kappa)) // 8) * 8
 
 
-def start_kernel(value, kappa, member, rows_f, cols_f, swap, windows):
+def start_kernel(
+    value_h, kappa_h, member_h, rows_h, cols_h, blocks_h, fold_h, swap, windows, value, kappa, member, rows_f, cols_f, blocks, fold, done
+):
     levels, rows, _ = value.shape
+    coarse = rows_f.shape[0]
     lev = lax.axis_index("lev")
+    sources = (member_h, cols_h, rows_h, kappa_h, value_h, blocks_h, fold_h)
+    targets = (member, cols_f, rows_f, kappa, value, blocks, fold)
+    copies = [pltpu.make_async_copy(s, t, done.at[i]) for i, (s, t) in enumerate(zip(sources, targets))]
+    for copy in copies:
+        copy.start()
+    for copy in copies[:3]:
+        copy.wait()
+    smoothed = dot_precise(rows_f[...], dot_precise(member[0], cols_f[...]))
+    windows[pl.ds(0, coarse, stride=2), :] = smoothed
+    ring = pltpu.roll(smoothed, coarse - 1, 0)
+    windows[pl.ds(1, coarse, stride=2), :] = jnp.where(iota(smoothed.shape, 0) == coarse - 1, smoothed, ring)
+    for copy in copies[3:]:
+        copy.wait()
     for j in range(STEPS):
         at = level_at(levels - 1 - j, levels, lev)
         k = kappa[at]
         swap[j * rows : (j + 1) * rows, :] = jnp.sqrt(k) * value[at]
         if j < STEPS - 1:
             swap[(STEPS + j) * rows : (STEPS + j + 1) * rows, :] = k
-    coarse = rows_f.shape[0]
-    shape = (2 * coarse, coarse)
-    pair = iota(shape, 0)
-    wanted = jnp.minimum(pair // 2 + pair % 2, coarse - 1)
-    pick = jnp.where(iota(shape, 1) == wanted, 1.0, 0.0).astype(F32)
-    right_done = dot_precise(member[0], cols_f[...])
-    windows[...] = dot_precise(dot_precise(pick, rows_f[...]), right_done)
 
 
 def pack_rows(plan, row_of, up, down, rows):
@@ -274,7 +283,7 @@
 
 
 def terms_kernel(perturbations, weighted, interp, sent, terms):
-    members, levels, rows, width = perturbations.shape
+    members, levels, rows, _ = perturbations.shape
     group = min(GROUP, members)
     scale = (members - 1) ** (-0.5)
     shape = (4 * group, group * rows)
@@ -282,7 +291,7 @@
     column = iota(shape, 1)
     fraction = (column % rows).astype(F32) * (1.0 / rows)
     share = jnp.where(pair % 2 == 0, 1.0 - fraction, fraction)
-    share = jnp.where(column // rows == pair // 4, share, 0.0)
+    share = jnp.where(column // rows == pair // 4, share, 0.0).astype(BF16)
     held = [weighted[l] for l in range(levels)]
 
     def one_group(first):
@@ -292,7 +301,8 @@
                 term = term + held[l] * perturbations[first + m, l].astype(F32)
             terms[m * rows : (m + 1) * rows, :] = term
         narrow = dot_split(terms[...], interp[...], ((1,), (1,)))
-        sent[pl.ds(pl.multiple_of(4 * first, 8), 4 * group), :] = scale * dot_precise(share, narrow)
+        narrow = sum_parts(narrow, lambda part: jnp.dot(share, part, preferred_element_type=F32))
+        sent[pl.ds(pl.multiple_of(4 * first, 8), 4 * group), :] = scale * narrow
 
     if members <= GROUP:
         one_group(0)
@@ -302,23 +312,31 @@
 
 def member_kernel(received, member, rows_f, cols_f, gradient):
     coarse = rows_f.shape[0]
-    shape = (coarse, received.shape[0])
-    source = iota(shape, 1)
-    wanted = jnp.minimum(source // 4 + source % 2, coarse - 1)
-    gather = jnp.where(iota(shape, 0) == wanted, 1.0, 0.0).astype(F32)
-    smooth = dot_precise(gather, received[...])
+    main, following = [
+        received[pl.ds(row, coarse, stride=4), :] + received[pl.ds(row + 2, coarse, stride=4), :] for row in range(2)
+    ]
+    at = iota(main.shape, 0)
+    smooth = main + jnp.where(at == 0, 0.0, pltpu.roll(following, 1, 0))
+    smooth = smooth + jnp.where(at == coarse - 1, following, 0.0)
     right_done = dot_precise(smooth, cols_f[...], ((1,), (1,)))
     gradient[0] = member[0] + dot_precise(rows_f[...], right_done, ((0,), (0,)))
 
 
-def call(kernel, outs, scratch=(), name=None, flops=100000):
-    return pl.pallas_call(
+def call(kernel, outs, scratch=(), results=(), staged=True):
+    run = pl.pallas_call(
         kernel,
-        out_shape=[jax.ShapeDtypeStruct(shape, dtype) for shape, dtype in outs],
-        scratch_shapes=[pltpu.VMEM(shape, dtype) for shape, dtype in scratch],
-        cost_estimate=pl.CostEstimate(flops=flops, transcendentals=0, bytes_accessed=0),
-        name=name,
+        out_shape=[
+            jax.ShapeDtypeStruct(shape, dtype) if i in results else pltpu.VMEM(shape, dtype)
+            for i, (shape, dtype) in enumerate(outs)
+        ],
+        scratch_shapes=[pltpu.VMEM(shape, dtype) for shape, dtype in scratch]
+        + ([] if staged else [pltpu.SemaphoreType.DMA((7,))]),
+        **({} if staged else {"in_specs": [pl.BlockSpec(memory_space=pltpu.HBM)] * 7}),
+        cost_estimate=pl.CostEstimate(flops=100000, transcendentals=0, bytes_accessed=0),
+        compiler_params=pltpu.CompilerParams(vmem_limit_bytes=VMEM_BYTES),
     )
+    space = pltpu.VMEM if staged else pltpu.HBM
+    return lambda *args: run(*[pltpu.with_memory_space_constraint(a, space) for a in args])
 
 
 def on_device(
@@ -341,14 +359,30 @@
     ring_down = [(j, i) for i, j in ring_up]
     partner = [(0, 1), (1, 0)]
     cell = (levels, rows, width)
-    fold = fold_map.reshape(1, width)
-    blocks = huber_blocks.reshape(levels, coarse)
-
-    swap, windows = call(
+
+    swap, windows, value, kappa, member, rows_f, cols_f, blocks, fold = call(
         start_kernel,
-        [(((2 * STEPS - 1) * rows, width), F32), ((2 * coarse_rows, coarse), F32)],
-        name="start",
-    )(static_control, diffusivity, member_control, rows_factor, column_factor)
+        [
+            (((2 * STEPS - 1) * rows, width), F32),
+            ((2 * coarse_rows, coarse), F32),
+            (cell, F32),
+            (cell, F32),
+            (member_control.shape, F32),
+            (rows_factor.shape, F32),
+            (column_factor.shape, F32),
+            ((levels, coarse), jnp.int32),
+            ((1, width), jnp.int32),
+        ],
+        staged=False,
+    )(
+        static_control,
+        diffusivity,
+        member_control,
+        rows_factor,
+        column_factor,
+        huber_blocks.reshape(levels, coarse),
+        fold_map.reshape(1, width),
+    )
     swap = lax.ppermute(swap, "lev", partner)
     windows = lax.all_to_all(windows.reshape(wide, 2, coarse), "wide", 0, 0, tiled=True)
     windows = windows.reshape(2 * members, coarse)
@@ -356,8 +390,7 @@
     up, down, interp, huber = call(
         pack_static_kernel,
         [((count, width), F32), ((count, width), F32), ((coarse, width), BF16), ((levels, width), F32)],
-        name="pack_static",
-    )(static_control, diffusivity, swap, blocks)
+    )(value, kappa, swap, blocks)
     low = lax.ppermute(up, "wide", ring_up)
     high = lax.ppermute(down, "wide", ring_down)
     entries = levels + STEPS
@@ -365,40 +398,30 @@
         static_kernel,
         [(cell, F32), ((entries - 1, 2 * rows, width), F32)],
         [((entries, 2 * rows, width), F32), (cell, F32), ((8, width), F32)],
-        name="diffuse_static",
-    )(static_control, diffusivity, swap, low, high, fold)
+    )(value, kappa, swap, low, high, fold)
     increment, weighted, scaled, swap = call(
         ensemble_kernel,
         [(cell, F32), (cell, F32), (cell, F32), ((STEPS * rows, width), F32)],
         [((2 * members, width), F32)],
-        name="ensemble",
-    )(windows, interp, perturbations, diffused, innovation, diffusivity, ocean_mask, huber)
+    )(windows, interp, perturbations, diffused, innovation, kappa, ocean_mask, huber)
     swap = lax.ppermute(swap, "lev", partner)
     (sent,) = call(
-        terms_kernel,
-        [((4 * members, coarse), F32)],
-        [((min(GROUP, members) * rows, width), F32)],
-        name="terms",
+        terms_kernel, [((4 * members, coarse), F32)], [((min(GROUP, members) * rows, width), F32)]
     )(perturbations, weighted, interp)
-    received = lax.all_to_all(
-        sent.reshape(2 * members, 2, coarse), ("wide", "lev"), 0, 0, tiled=True
-    ).reshape(4 * members, coarse)
+    received = lax.all_to_all(sent.reshape(2 * members, 2, coarse), ("wide", "lev"), 0, 0, tiled=True)
+    received = received.reshape(4 * members, coarse)
     count = padded_rows(levels, False)
-    up, down = call(
-        pack_weighted_kernel,
-        [((count, width), F32), ((count, width), F32)],
-        name="pack_weighted",
-    )(scaled, swap)
+    up, down = call(pack_weighted_kernel, [((count, width), F32), ((count, width), F32)])(scaled, swap)
     low = lax.ppermute(up, "wide", ring_up)
     high = lax.ppermute(down, "wide", ring_down)
     (static_gradient,) = call(
         weighted_kernel,
         [(cell, F32)],
         [((entries, 2 * rows, width), F32), ((8, LANES), F32), (cell, F32), ((8, width), F32)],
-        name="diffuse_weighted",
-    )(static_control, weighted, diffusivity, kappa_ext, scaled, swap, low, high, fold)
-    (member_gradient,) = call(member_kernel, [(member_control.shape, F32)], name="member")(
-        received, member_control, rows_factor, column_factor
+        results=(0,),
+    )(value, weighted, kappa, kappa_ext, scaled, swap, low, high, fold)
+    (member_gradient,) = call(member_kernel, [(member_control.shape, F32)], results=(0,))(
+        received, member, rows_f, cols_f
     )
     return (increment, member_gradient, static_gradient)
 

time: 60.7 us -> 48.2 us (0.79)
  Pallas kernels: 18.2 us -> 7.24 us
  blocking collectives: 10.4 us -> 0 us
  waiting for transfers between devices: 10.7 us -> 19.4 us
  starting transfers between devices: 17.1 us -> 19.9 us
  local copies, waits for them, and re-layouts: 3.18 us -> 0.67 us
    pallas_call x8, Pallas kernels: 18.2 us -> 7.24 us  [call(): run(*[pltpu.with_memory_space_constraint(a, space) for a in args])]
    all_to_all x1 -> x0, blocking collectives: 10.4 us -> none  [on_device(): lax.all_to_all(sent.reshape(2 * members, 2, coarse), ('wide', 'lev'), 0,...]
    all_to_all x0 -> x1, waiting for transfers between devices: none -> 6.7 us  [on_device(): lax.all_to_all(sent.reshape(2 * members, 2, coarse), ('wide', 'lev'), 0,...]
    all_to_all x0 -> x1, starting transfers between devices: none -> 2.57 us  [on_device(): lax.all_to_all(sent.reshape(2 * members, 2, coarse), ('wide', 'lev'), 0,...]
    unnamed x14 -> x7, local copies, waits for them, and re-layouts: 3.18 us -> 0.67 us
    all_to_all x1, waiting for transfers between devices: 3.18 us -> 5.63 us  [on_device(): lax.all_to_all(windows.reshape(wide, 2, coarse), 'wide', 0, 0, tiled=True)]
  transfers between devices with their start and end apart: 7 -> 8, of which waited for: 3 -> 4; matrix products, arithmetic and copies ran while one was open for 0% -> 1% of each run, Pallas kernels for 12% -> 6%
where the time goes in v2:
time: 48.2 us; the launch traced here: 47.9 us
  starting transfers between devices  19.9 us (41%)
  waiting for transfers between devices  19.4 us (40%)
  Pallas kernels  7.24 us (15%)
  between operations  0.74 us (2%)
  local copies, waits for them, and re-layouts  0.67 us (1%)
    ppermute x2, starting transfers between devices, on_device(): high = lax.ppermute(down, 'wide', ring_down)  8.87 us
    pallas_call x8, Pallas kernels, call(): run(*[pltpu.with_memory_space_constraint(a, space) for a in args])  7.24 us
    ppermute x2, waiting for transfers between devices, on_device(): swap = lax.ppermute(swap, 'lev', partner)  7.08 us
    all_to_all x1, waiting for transfers between devices, on_device(): lax.all_to_all(sent.reshape(2 * members, 2, coarse), ('wide', 'lev'), 0,...  6.7 us
    all_to_all x1, waiting for transfers between devices, on_device(): lax.all_to_all(windows.reshape(wide, 2, coarse), 'wide', 0, 0, tiled=True)  5.63 us
    ppermute x2, starting transfers between devices, on_device(): swap = lax.ppermute(swap, 'lev', partner)  4.86 us
    all_to_all x1, starting transfers between devices, on_device(): lax.all_to_all(windows.reshape(wide, 2, coarse), 'wide', 0, 0, tiled=True)  3.49 us
    all_to_all x1, starting transfers between devices, on_device(): lax.all_to_all(sent.reshape(2 * members, 2, coarse), ('wide', 'lev'), 0,...  2.57 us
  transfers between devices with their start and end apart: 8, of which 4 were waited for; matrix products, arithmetic and copies ran while one was open for 1% of the time, Pallas kernels for 6%

profile of v2, /device:TPU:0, one launch (start us, length us, event | category | flops | bytes accessed | tf_op | source)
XLA Modules:
  0.0 47.9 jit_solution(2461290614345885156)
XLA Ops:
  0.6 0.0 copy-start
  0.6 1.9 %shard_map.121 = (f32[40,1024]{1,0:T(8,128)S(1)}, f32[32,128]{1,0:T(8,128)}, f32[4,8,1024]{2,1,0:T(8,128)S(1)}, f32[4,8,1024]{2,1,0:T(8,128)S(1)}, f32[1,16,128]...) custom-call(f32[4,8,1024]{2,1,0:T(8,128)} %value_h.1, ...), custom_call_target="tpu_custom_call" | custom-call | flops 100000 | tf_op jit(solution)/shard_map/pallas_call | solution.py:339
  2.6 3.1 %collective-permute-start = (f32[40,1024]{1,0:T(8,128)S(1)}, f32[40,1024]{1,0:T(8,128)S(1)}, u32[]{:S(2)}, u32[]{:S(2)}) collective-permute-start(f32[40,1024]{1,0:T(8,128)S(1)} %get-tuple-element.27), channel_id=1, source_target_pairs={{0,1},{1,0},{2,3},{3,2},{4,5},{5,4},{6,7},{7,6},{8,9},{9,8},{10,11... | collective-permute-start | bytes 491528 | tf_op jit(solution)/shard_map/ppermute | solution.py:386
  5.6 4.2 %collective-permute-done.swap = f32[40,1024]{1,0:T(8,128)S(1)} collective-permute-done((f32[40,1024]{1,0:T(8,128)S(1)}, f32[40,1024]{1,0:T(8,128)S(1)}, u32[]{:S(2)}, u32[]{:S(2)}) %collective-permute-start) | collective-permute-done | bytes 163872 | tf_op jit(solution)/shard_map/ppermute | solution.py:386
  9.8 0.2 shard_map.122
  10.1 0.0 collective-permute-start.1
  10.1 4.4 %collective-permute-start.2 = (f32[24,1024]{1,0:T(8,128)S(1)}, f32[24,1024]{1,0:T(8,128)S(1)}, u32[]{:S(2)}, u32[]{:S(2)}) collective-permute-start(f32[24,1024]{1,0:T(8,128)S(1)} %get-tuple-element.31), channel_id=1, source_target_pairs={{2,0},{4,2},{6,4},{8,6},{10,8},{12,10},{14,12},{16,14},{18,16},{20... | collective-permute-start | bytes 294920 | tf_op jit(solution)/shard_map/ppermute | solution.py:395
  14.5 3.5 %all-to-all-start = ((f32[16,2,128]{2,1,0:T(2,128)}), f32[16,2,128]{2,1,0:T(2,128)S(1)}, u32[]{:S(2)}, u32[]{:S(2)}) async-start(f32[16,2,128]{2,1,0:T(2,128)} %bitcast.2), calls=%async_computation | async-start | bytes 32768 | tf_op jit(solution)/shard_map/all_to_all | solution.py:387
  18.0 0.0 collective-permute-done.1.low
  18.0 0.0 collective-permute-done.2.high
  18.0 0.0 copy-start.1
  18.0 0.0 copy-start.2
  18.1 0.8 %shard_map.123 = (f32[4,8,1024]{2,1,0:T(8,128)S(1)}, f32[6,16,1024]{2,1,0:T(8,128)S(1)}) custom-call(f32[4,8,1024]{2,1,0:T(8,128)S(1)} %get-tuple-element.25.value, f32[4,8,1024]{2,1,0:T(8,128)S(1)} %get-tuple-element.26.kappa, f32[40,1024]{1,0:T(8,128)S(1)} %collective-permute-done.swap, f32[24,1024]{1,0:T(8,128)S(1)} %collective-permute-done.1.low, ...), custom_call_target="tpu_custom_call" | custom-call | flops 100000 | tf_op jit(solution)/shard_map/pallas_call | solution.py:339
  18.8 5.6 %all-to-all-done = f32[16,2,128]{2,1,0:T(2,128)S(1)} async-done(((f32[16,2,128]{2,1,0:T(2,128)}), f32[16,2,128]{2,1,0:T(2,128)S(1)}, u32[]{:S(2)}, u32[]{:S(2)}) %all-to-all-start) | async-done | bytes 16416 | tf_op jit(solution)/shard_map/all_to_all | solution.py:387
  24.5 0.0 copy-done
  24.5 0.0 copy-done.1
  24.5 0.0 copy-done.2
  24.5 0.6 %shard_map.124 = (f32[4,8,1024]{2,1,0:T(8,128)S(1)}, f32[4,8,1024]{2,1,0:T(8,128)S(1)}, f32[4,8,1024]{2,1,0:T(8,128)S(1)}, f32[24,1024]{1,0:T(8,128)S(1)}) custom-call(f32[32,128]{1,0:T(8,128)S(1)} %bitcast.7, bf16[128,1024]{1,0:T(8,128)(2,1)S(1)} %get-tuple-element.29.interp, bf16[16,4,8,1024]{3,2,1,0:T(8,128)(2,1)S(1)} %copy-done, ...), custom_call_target="tpu_custom_call" | custom-call | flops 100000 | tf_op jit(solution)/shard_map/pallas_call | solution.py:339
  25.1 1.8 %collective-permute-start.3 = (f32[24,1024]{1,0:T(8,128)S(1)}, f32[24,1024]{1,0:T(8,128)S(1)}, u32[]{:S(2)}, u32[]{:S(2)}) collective-permute-start(f32[24,1024]{1,0:T(8,128)S(1)} %get-tuple-element.42), channel_id=1, source_target_pairs={{0,1},{1,0},{2,3},{3,2},{4,5},{5,4},{6,7},{7,6},{8,9},{9,8},{10,11... | collective-permute-start | bytes 294920 | tf_op jit(solution)/shard_map/ppermute | solution.py:407
  26.9 2.9 %collective-permute-done.3.swap = f32[24,1024]{1,0:T(8,128)S(1)} collective-permute-done((f32[24,1024]{1,0:T(8,128)S(1)}, f32[24,1024]{1,0:T(8,128)S(1)}, u32[]{:S(2)}, u32[]{:S(2)}) %collective-permute-start.3) | collective-permute-done | bytes 98336 | tf_op jit(solution)/shard_map/ppermute | solution.py:407
  29.8 0.1 collective-permute-start.4
  29.9 4.4 %collective-permute-start.5 = (f32[16,1024]{1,0:T(8,128)S(1)}, f32[16,1024]{1,0:T(8,128)S(1)}, u32[]{:S(2)}, u32[]{:S(2)}) collective-permute-start(f32[16,1024]{1,0:T(8,128)S(1)} %get-tuple-element.44), channel_id=1, source_target_pairs={{2,0},{4,2},{6,4},{8,6},{10,8},{12,10},{14,12},{16,14},{18,16},{20... | collective-permute-start | bytes 196616 | tf_op jit(solution)/shard_map/ppermute | solution.py:416
  34.3 1.3 %shard_map.125 = f32[64,128]{1,0:T(8,128)} custom-call(bf16[16,4,8,1024]{3,2,1,0:T(8,128)(2,1)S(1)} %copy-done, f32[4,8,1024]{2,1,0:T(8,128)S(1)} %get-tuple-element.36.weighted, bf16[128,1024]{1,0:T(8,128)(2,1)S(1)} %get-tuple-element.29.interp), custom_call_target="tpu_custom_call" | custom-call | flops 100000 | tf_op jit(solution)/shard_map/pallas_call | solution.py:339
  35.7 2.6 %all-to-all-start.1 = ((f32[32,2,128]{2,1,0:T(2,128)}), f32[32,2,128]{2,1,0:T(2,128)S(1)}, u32[]{:S(2)}, u32[]{:S(2)}) async-start(f32[32,2,128]{2,1,0:T(2,128)} %bitcast.4), calls=%async_computation.1 | async-start | bytes 65536 | tf_op jit(solution)/shard_map/all_to_all | solution.py:411
  38.2 0.7 %copy.13 = f32[4,8,1024]{2,1,0:T(8,128)} copy(f32[4,8,1024]{2,1,0:T(8,128)S(1)} %get-tuple-element.45) | data formatting | bytes 262144
  38.9 6.7 %all-to-all-done.1 = f32[32,2,128]{2,1,0:T(2,128)S(1)} async-done(((f32[32,2,128]{2,1,0:T(2,128)}), f32[32,2,128]{2,1,0:T(2,128)S(1)}, u32[]{:S(2)}, u32[]{:S(2)}) %all-to-all-start.1) | async-done | bytes 32800 | tf_op jit(solution)/shard_map/all_to_all | solution.py:411
  45.6 0.9 %shard_map.126 = f32[1,16,128]{2,1,0:T(8,128)} custom-call(f32[64,128]{1,0:T(8,128)S(1)} %bitcast.6, f32[1,16,128]{2,1,0:T(8,128)S(1)} %get-tuple-element.37.member, f32[16,16]{1,0:T(8,128)S(1)} %get-tuple-element.38.rows_f, f32[128,128]{1,0:T(8,128)S(1)} %get-tuple-element.39.cols_f), custom_call_target="tpu_custom_call" | custom-call | flops 100000 | tf_op jit(solution)/shard_map/pallas_call | solution.py:339
  46.5 0.0 collective-permute-done.4.low
  46.5 0.0 collective-permute-done.5.high
  46.5 1.4 %shard_map.128 = f32[4,8,1024]{2,1,0:T(8,128)} custom-call(f32[4,8,1024]{2,1,0:T(8,128)S(1)} %get-tuple-element.25.value, f32[4,8,1024]{2,1,0:T(8,128)S(1)} %get-tuple-element.36.weighted, f32[4,8,1024]{2,1,0:T(8,128)S(1)} %get-tuple-element.26.kappa, f32[6,16,1024]{2,1,0:T(8,128)S(1)} %get-tuple-element.40.kappa_ext, ...), custom_call_target="tpu_custom_call" | custom-call | flops 100000 | tf_op jit(solution)/shard_map/pallas_call | solution.py:339
  (1 shorter events, 0.0 us)
Async XLA Ops:
  0.6 23.8 %copy-start = (bf16[16,4,8,1024]{3,2,1,0:T(8,128)(2,1)S(1)}, bf16[16,4,8,1024]{3,2,1,0:T(8,128)(2,1)}, u32[]{:S(2)}) copy-start(bf16[16,4,8,1024]{3,2,1,0:T(8,128)(2,1)} %perturbations.3) | copy-start | bytes 3145732
  2.6 7.3 %collective-permute-start = (f32[40,1024]{1,0:T(8,128)S(1)}, f32[40,1024]{1,0:T(8,128)S(1)}, u32[]{:S(2)}, u32[]{:S(2)}) collective-permute-start(f32[40,1024]{1,0:T(8,128)S(1)} %get-tuple-element.27), channel_id=1, source_target_pairs={{0,1},{1,0},{2,3},{3,2},{4,5},{5,4},{6,7},{7,6},{8,9},{9,8},{10,11... | collective-permute-start | bytes 491528 | tf_op jit(solution)/shard_map/ppermute | solution.py:386
  10.1 8.0 %collective-permute-start.1 = (f32[24,1024]{1,0:T(8,128)S(1)}, f32[24,1024]{1,0:T(8,128)S(1)}, u32[]{:S(2)}, u32[]{:S(2)}) collective-permute-start(f32[24,1024]{1,0:T(8,128)S(1)} %get-tuple-element.30), channel_id=1, source_target_pairs={{0,2},{2,4},{4,6},{6,8},{8,10},{10,12},{12,14},{14,16},{16,18},{18... | collective-permute-start | bytes 294920 | tf_op jit(solution)/shard_map/ppermute | solution.py:394
  10.1 8.0 %collective-permute-start.2 = (f32[24,1024]{1,0:T(8,128)S(1)}, f32[24,1024]{1,0:T(8,128)S(1)}, u32[]{:S(2)}, u32[]{:S(2)}) collective-permute-start(f32[24,1024]{1,0:T(8,128)S(1)} %get-tuple-element.31), channel_id=1, source_target_pairs={{2,0},{4,2},{6,4},{8,6},{10,8},{12,10},{14,12},{16,14},{18,16},{20... | collective-permute-start | bytes 294920 | tf_op jit(solution)/shard_map/ppermute | solution.py:395
  14.5 10.0 %all-to-all-start = ((f32[16,2,128]{2,1,0:T(2,128)}), f32[16,2,128]{2,1,0:T(2,128)S(1)}, u32[]{:S(2)}, u32[]{:S(2)}) async-start(f32[16,2,128]{2,1,0:T(2,128)} %bitcast.2), calls=%async_computation | async-start | bytes 32768 | tf_op jit(solution)/shard_map/all_to_all | solution.py:387
  18.0 6.4 %copy-start.1 = (f32[4,8,1024]{2,1,0:T(8,128)S(1)}, f32[4,8,1024]{2,1,0:T(8,128)}, u32[]{:S(2)}) copy-start(f32[4,8,1024]{2,1,0:T(8,128)} %innovation.1) | copy-start | bytes 393220
  18.0 6.4 %copy-start.2 = (s32[8,1024]{1,0:T(8,128)S(1)}, s32[8,1024]{1,0:T(8,128)}, u32[]{:S(2)}) copy-start(s32[8,1024]{1,0:T(8,128)} %mask.1) | copy-start | bytes 98308
  25.1 4.7 %collective-permute-start.3 = (f32[24,1024]{1,0:T(8,128)S(1)}, f32[24,1024]{1,0:T(8,128)S(1)}, u32[]{:S(2)}, u32[]{:S(2)}) collective-permute-start(f32[24,1024]{1,0:T(8,128)S(1)} %get-tuple-element.42), channel_id=1, source_target_pairs={{0,1},{1,0},{2,3},{3,2},{4,5},{5,4},{6,7},{7,6},{8,9},{9,8},{10,11... | collective-permute-start | bytes 294920 | tf_op jit(solution)/shard_map/ppermute | solution.py:407
  29.8 16.7 %collective-permute-start.4 = (f32[16,1024]{1,0:T(8,128)S(1)}, f32[16,1024]{1,0:T(8,128)S(1)}, u32[]{:S(2)}, u32[]{:S(2)}) collective-permute-start(f32[16,1024]{1,0:T(8,128)S(1)} %get-tuple-element.43), channel_id=1, source_target_pairs={{0,2},{2,4},{4,6},{6,8},{8,10},{10,12},{12,14},{14,16},{16,18},{18... | collective-permute-start | bytes 196616 | tf_op jit(solution)/shard_map/ppermute | solution.py:415
  29.9 16.6 %collective-permute-start.5 = (f32[16,1024]{1,0:T(8,128)S(1)}, f32[16,1024]{1,0:T(8,128)S(1)}, u32[]{:S(2)}, u32[]{:S(2)}) collective-permute-start(f32[16,1024]{1,0:T(8,128)S(1)} %get-tuple-element.44), channel_id=1, source_target_pairs={{2,0},{4,2},{6,4},{8,6},{10,8},{12,10},{14,12},{16,14},{18,16},{20... | collective-permute-start | bytes 196616 | tf_op jit(solution)/shard_map/ppermute | solution.py:416
  35.7 9.9 %all-to-all-start.1 = ((f32[32,2,128]{2,1,0:T(2,128)}), f32[32,2,128]{2,1,0:T(2,128)S(1)}, u32[]{:S(2)}, u32[]{:S(2)}) async-start(f32[32,2,128]{2,1,0:T(2,128)} %bitcast.4), calls=%async_computation.1 | async-start | bytes 65536 | tf_op jit(solution)/shard_map/all_to_all | solution.py:411
